TPU v7x, 8 devices: a whole 2x2x1 slice. The times are simulated.
8 devices in a mesh: dp: 1 (over z), tp: 8 (over y, x, core).
Axes of the slice: x: 2, y: 2, z: 1, core: 2. Of those that a mesh axis runs over, the one named last changes fastest.
Arguments:
- hidden: bfloat16 [256, 4, 8192], P('dp')
- w_head: bfloat16 [8192, 32000], P(None, 'tp')
- q_draft: float32 [256, 3, 32000], P(('dp', 'tp'))
- x_draft: int32 [256, 3], P('dp')
Outputs:
- output 1: float32 [256, 3], P(('dp', 'tp'))
- output 2: float32 [256], P(('dp', 'tp'))
- output 3: float32 [256, 3, 32000], P(('dp', 'tp'))
- output 4: float32 [256, 32000], P(('dp', 'tp'))
All inputs are finite; a program needn't handle non-finite values.
Results may differ from a plain program's by a relative error of at most 0.001.
Values are sent between devices in bfloat16 or wider.
A program may use at most 1 GiB of HBM per device.

v0:
```python
import jax
import jax.numpy as jnp
from jax import lax
from jax.sharding import PartitionSpec as P

INV_TEMP = 1.25


def verify_rows(logits, q_rows, x_rows):
    draft_len = q_rows.shape[1]
    row_peak = jnp.max(logits, axis=-1, keepdims=True)
    exp_vals = jnp.exp(logits - row_peak)
    target_p = exp_vals / jnp.sum(exp_vals, axis=-1, keepdims=True)
    draft_p = target_p[:, :draft_len]
    p_pick = jnp.take_along_axis(draft_p, x_rows[:, :, None], axis=2)[:, :, 0]
    q_pick = jnp.take_along_axis(q_rows, x_rows[:, :, None], axis=2)[:, :, 0]
    accept = jnp.minimum(1.0, p_pick / q_pick)
    expected = jnp.sum(jnp.cumprod(accept, axis=1), axis=1)
    excess = jnp.maximum(draft_p - q_rows, 0.0)
    residual = excess / jnp.sum(excess, axis=-1, keepdims=True)
    return accept, expected, residual, target_p[:, draft_len]


def solution(mesh):
    def local_step(hidden, w_shard, q_rows, x_group):
        seq_dev = q_rows.shape[0]
        logits = jnp.einsum("bjd,dv->bjv", hidden, w_shard, preferred_element_type=jnp.float32) * INV_TEMP
        seq_logits = lax.all_to_all(logits, "tp", 0, 2, tiled=True)
        tp_rank = lax.axis_index("tp")
        x_rows = lax.dynamic_slice_in_dim(x_group, tp_rank * seq_dev, seq_dev, axis=0)
        return verify_rows(seq_logits, q_rows, x_rows)

    return jax.shard_map(local_step, mesh=mesh,
                         in_specs=(P("dp", None, None), P(None, "tp"), P(("dp", "tp"), None, None), P("dp", None)),
                         out_specs=(P(("dp", "tp"), None), P(("dp", "tp")), P(("dp", "tp"), None, None), P(("dp", "tp"), None)),
                         check_vma=False)
```

profile of v0, /device:TPU:0, one launch (start us, length us, event | category | flops | bytes accessed | tf_op | source)
XLA Modules:
  0.0 415.0 jit_solution(1240739804209597665)
XLA Ops:
  0.6 91.4 %fusion.3 = f32[256,4,4000]{0,2,1:T(8,128)} fusion(bf16[8192,4000]{0,1:T(8,128)(2,1)} %param.7, bf16[256,4,8192]{2,1,0:T(4,128)(2,1)} %param.6), kind=kOutput, calls=%fused_computation.8 | convolution fusion | flops 67112960000 | bytes 98697216 | tf_op jit(solution)/shard_map/bjd,dv->bjv/dot_general | solution.py:27
  92.1 20.2 %copy.26 = f32[256,4,4000]{2,1,0:T(4,128)} copy(f32[256,4,4000]{0,2,1:T(8,128)} %fusion.3) | data formatting | bytes 32768000 | tf_op jit(solution)/shard_map/mul | solution.py:27
  112.2 0.0 copy-start.2
  112.2 4.8 %all-to-all-start = ((f32[256,4,4000]{2,1,0:T(4,128)}), f32[256,4,4000]{2,1,0:T(4,128)}, u32[]{:S(2)}, u32[]{:S(2)}) async-start(f32[256,4,4000]{2,1,0:T(4,128)} %copy.26), calls=%async_computation | async-start | bytes 33554432 | tf_op jit(solution)/shard_map/all_to_all | solution.py:28
  117.1 0.0 copy-done.2
  117.1 0.1 fusion.14
  117.2 0.1 copy.30
  117.3 0.1 reshape.51
  117.4 3.6 gather_fusion.1
  121.0 0.1 reshape.60
  121.1 0.1 copy.34
  121.2 180.9 %all-to-all-done = f32[256,4,4000]{2,1,0:T(4,128)} async-done(((f32[256,4,4000]{2,1,0:T(4,128)}), f32[256,4,4000]{2,1,0:T(4,128)}, u32[]{:S(2)}, u32[]{:S(2)}) %all-to-all-start) | async-done | bytes 16384032 | tf_op jit(solution)/shard_map/all_to_all | solution.py:28
  302.1 15.2 %copy.27 = f32[256,4,4000]{2,0,1:T(8,128)S(1)} copy(f32[256,4,4000]{2,1,0:T(4,128)} %all-to-all-done) | data formatting | bytes 32768000 | tf_op jit(solution)/shard_map/all_to_all | solution.py:28
  317.3 0.0 copy-start
  317.3 5.7 %copy-done = f32[256,4,4000]{2,0,1:T(8,128)} copy-done((f32[256,4,4000]{2,0,1:T(8,128)}, f32[256,4,4000]{2,0,1:T(8,128)S(1)}, u32[]{:S(2)}) %copy-start) | copy-done | bytes 16384024
  323.0 11.7 %copy.28 = f32[32,4,8,4000]{3,2,0,1:T(8,128)} copy(f32[32,4,8,4000]{3,0,2,1:T(8,128)S(1)} %bitcast.30) | data formatting | bytes 32768000 | tf_op jit(solution)/shard_map/all_to_all | solution.py:28
  334.7 6.7 %reduce_max.9 = f32[32,4]{0,1:T(4,128)S(1)} reduce(f32[32,4,8,4000]{3,0,2,1:T(8,128)} %bitcast.31, f32[]{:T(128)} %constant.4.clone.1), dimensions={2,3}, to_apply=%region_0.0 | reduce | flops 4095872 | bytes 16384516 | tf_op jit(solution)/shard_map/reduce_max | solution.py:11
  341.5 8.3 %exponential_reduce_fusion = f32[32,4]{0,1:T(4,128)S(1)} fusion(f32[32,4,8,4000]{3,0,2,1:T(8,128)} %bitcast.32, f32[32,4]{0,1:T(4,128)S(1)} %reduce_max.9), kind=kLoop, calls=%fused_computation.5 | loop fusion | flops 8191872 | bytes 16385024 | tf_op jit(solution)/shard_map/reduce_sum | solution.py:13
  349.7 17.2 %all_to_all.16 = f32[32,4,32000]{2,0,1:T(8,128)} reshape(f32[32,4,8,4000]{3,2,0,1:T(8,128)} %copy.28) | data formatting | bytes 32768000 | tf_op jit(solution)/shard_map/all_to_all | solution.py:28
  366.9 11.8 %exponential_divide_fusion = f32[32,4,32000]{2,0,1:T(8,128)} fusion(f32[32,4,32000]{2,0,1:T(8,128)} %all_to_all.16, f32[32,4]{0,1:T(4,128)S(1)} %exponential_reduce_fusion, f32[32,4]{0,1:T(4,128)S(1)} %reduce_max.9), kind=kLoop, calls=%fused_computation.6 | loop fusion | flops 8192000 | bytes 32769024 | tf_op jit(solution)/shard_map/div | solution.py:13
  378.7 9.4 %fusion.8 = f32[32,3]{0,1:T(4,128)S(1)} fusion(f32[32,3,32000]{2,0,1:T(8,128)} %param.8, f32[32,4,32000]{2,0,1:T(8,128)} %exponential_divide_fusion), kind=kLoop, calls=%fused_computation.10 | loop fusion | flops 9215904 | bytes 24576384 | tf_op jit(solution)/shard_map/reduce_sum | solution.py:20
  388.0 4.4 %slice_bitcast_fusion = f32[32,32000]{1,0:T(8,128)} fusion(f32[32,4,32000]{2,0,1:T(8,128)} %exponential_divide_fusion), kind=kLoop, calls=%fused_computation.11 | loop fusion | bytes 8192000 | tf_op jit(solution)/shard_map/squeeze | solution.py:21
  392.4 18.0 %broadcast_divide_fusion = (f32[32,3,32000]{2,0,1:T(8,128)}, f32[32,3,32000]{2,0,1:T(8,128)}) fusion(f32[32,3]{0,1:T(4,128)S(1)} %fusion.8, f32[32,3,32000]{2,0,1:T(8,128)} %param.8, f32[32,4,32000]{2,0,1:T(8,128)} %exponential_divide_fusion), kind=kLoop, calls=%fused_computation.9 | loop fusion | flops 9216000 | bytes 49152384 | tf_op jit(solution)/shard_map/div | solution.py:20
  410.5 3.6 gather_fusion
  414.1 0.1 reshape.54
  414.2 0.1 copy.31
  414.3 0.1 minimum_bitcast_fusion
  414.4 0.0 copy-start.1
  414.4 0.5 reduce_sum.28
  415.0 0.0 copy-done.1
  (5 shorter events, 0.1 us)
Async XLA Ops:
  112.2 4.8 %copy-start.2 = (s32[256,3]{0,1:T(4,128)S(1)}, s32[256,3]{0,1:T(4,128)}, u32[]{:S(2)}) copy-start(s32[256,3]{0,1:T(4,128)} %param.9) | copy-start | bytes 9220
  112.2 189.8 %all-to-all-start = ((f32[256,4,4000]{2,1,0:T(4,128)}), f32[256,4,4000]{2,1,0:T(4,128)}, u32[]{:S(2)}, u32[]{:S(2)}) async-start(f32[256,4,4000]{2,1,0:T(4,128)} %copy.26), calls=%async_computation | async-start | bytes 33554432 | tf_op jit(solution)/shard_map/all_to_all | solution.py:28
  317.3 5.7 %copy-start = (f32[256,4,4000]{2,0,1:T(8,128)}, f32[256,4,4000]{2,0,1:T(8,128)S(1)}, u32[]{:S(2)}) copy-start(f32[256,4,4000]{2,0,1:T(8,128)S(1)} %copy.27) | copy-start | bytes 49152004
  414.4 0.6 copy-start.1
where the time goes:
time: 416 us; the launch traced here: 415 us
  waiting for transfers between devices  181 us (44%)
  matrix products  91.4 us (22%)
  local copies, waits for them, and re-layouts  82.2 us (20%)
  other arithmetic  55 us (13%)
  starting transfers between devices  4.8 us (1%)
    all_to_all x1, waiting for transfers between devices, local_step(): seq_logits = lax.all_to_all(logits, 'tp', 0, 2, tiled=True)  181 us
    dot_general x1, matrix products, local_step(): jnp.einsum('bjd,dv->bjv', hidden, w_shard, preferred_element_type=jnp.flo...  91.4 us
    all_to_all x3, local copies, waits for them, and re-layouts, local_step(): seq_logits = lax.all_to_all(logits, 'tp', 0, 2, tiled=True)  44.1 us
    mul x1, local copies, waits for them, and re-layouts, local_step(): jnp.einsum('bjd,dv->bjv', hidden, w_shard, preferred_element_type=jnp.flo...  20.2 us
    div x1, other arithmetic, verify_rows(): residual = excess / jnp.sum(excess, axis=-1, keepdims=True)  18 us
    div x1, other arithmetic, verify_rows(): target_p = exp_vals / jnp.sum(exp_vals, axis=-1, keepdims=True)  11.8 us
    reduce_sum x1, other arithmetic, verify_rows(): residual = excess / jnp.sum(excess, axis=-1, keepdims=True)  9.37 us
  transfers between devices with their start and end apart: 1, of which 1 were waited for; matrix products, arithmetic and copies ran while one was open for 1% of the time, Pallas kernels for 0%

commit v1 on v0

v1 whole, which is shorter than its diff:
```python
import functools

import jax
import jax.numpy as jnp
from jax import lax
from jax.experimental import pallas as pl
from jax.experimental.pallas import tpu as pltpu
from jax.sharding import PartitionSpec as P

INV_TEMP = 1.25
MESH = pl.DeviceIdType.MESH
LANE = 128
TILE = 256
HALVES = 2
SLOTS = 3
ORDER = (6, 2, 4, 7, 3, 5, 1)


def peer_of(me, k):
    d = me
    for bit in (1, 2, 4):
        if k & bit:
            d = d + bit * (1 - 2 * ((me // bit) % 2))
    return d


def logits_kernel(h_ref, w_ref, recv_ref, h_buf, w_buf, send_buf, h_sem, w_sem, own_sem, send_sem, recv_sem):
    me = lax.axis_index("tp")
    vocab = w_ref.shape[0]
    rows = h_buf.shape[1]
    seg = rows // 8
    n_tiles = pl.cdiv(vocab, TILE)
    last = vocab - (n_tiles - 1) * TILE
    lt = TILE // LANE

    def w_copy(t, size):
        slot = lax.rem(t, SLOTS)
        return pltpu.make_async_copy(w_ref.at[pl.ds(pl.multiple_of(t * TILE, TILE), size)], w_buf.at[slot, pl.ds(0, size)], w_sem.at[slot])

    def w_start(t):
        @pl.when(t < n_tiles - 1)
        def _():
            w_copy(t, TILE).start()

        @pl.when(t == n_tiles - 1)
        def _():
            w_copy(t, last).start()

    def w_wait(t):
        @pl.when(t < n_tiles - 1)
        def _():
            w_copy(t, TILE).wait()

        @pl.when(t == n_tiles - 1)
        def _():
            w_copy(t, last).wait()

    def h_start(half):
        for d in range(8):
            src = h_ref.at[pl.ds((d * HALVES + half) * seg, seg)]
            pltpu.make_async_copy(src, h_buf.at[half, pl.ds(d * seg, seg)], h_sem.at[half]).start()

    def h_wait(half):
        pltpu.make_async_copy(h_ref.at[pl.ds(0, rows)], h_buf.at[half], h_sem.at[half]).wait()

    h_start(0)
    w_copy(0, TILE).start()
    h_start(1)
    w_copy(1, TILE).start()

    barrier = pltpu.get_barrier_semaphore()
    for k in range(1, 8):
        pl.semaphore_signal(barrier, inc=1, device_id={"tp": peer_of(me, k)}, device_id_type=MESH)
    pl.semaphore_wait(barrier, 7)

    def step(i, carry):
        t = i // HALVES
        half = lax.rem(i, HALVES)
        slot = lax.rem(t, SLOTS)

        @pl.when(half == 0)
        def _():
            w_wait(t)

            @pl.when(t + 2 < n_tiles)
            def _():
                w_start(t + 2)

        @pl.when(i == 0)
        def _():
            h_wait(0)

        @pl.when(i == 1)
        def _():
            h_wait(1)

        z = lax.dot_general(h_buf[half], w_buf[slot], (((1,), (1,)), ((), ())), preferred_element_type=jnp.float32) * INV_TEMP
        for c in range(lt):
            send_buf[i, c] = z[:, c * LANE:(c + 1) * LANE]
        for k in ORDER:
            d = peer_of(me, k)
            pltpu.make_async_remote_copy(
                src_ref=send_buf.at[i, :, pl.ds(pl.multiple_of(d * seg, seg), seg)],
                dst_ref=recv_ref.at[me, pl.ds(t * lt, lt), half],
                send_sem=send_sem.at[k - 1],
                recv_sem=recv_sem.at[k - 1],
                device_id={"tp": d},
                device_id_type=MESH,
            ).start()
        pltpu.make_async_copy(
            send_buf.at[i, :, pl.ds(pl.multiple_of(me * seg, seg), seg)],
            recv_ref.at[me, pl.ds(t * lt, lt), half],
            own_sem.at[0],
        ).start()
        return carry

    lax.fori_loop(0, n_tiles * HALVES, step, 0)

    pltpu.make_async_copy(recv_ref.at[me], recv_ref.at[me], own_sem.at[0]).wait()
    for k in ORDER:
        d = peer_of(me, k)
        done = pltpu.make_async_remote_copy(
            src_ref=recv_ref.at[d],
            dst_ref=recv_ref.at[d],
            send_sem=send_sem.at[k - 1],
            recv_sem=recv_sem.at[k - 1],
            device_id={"tp": d},
            device_id_type=MESH,
        )
        done.wait_send()
        done.wait_recv()


def verify_kernel(x_ref, z_ref, q_ref, res_ref, bonus_ref, acc_ref, exp_ref):
    i = pl.program_id(0)
    n_src, n_lt = z_ref.shape[0], z_ref.shape[1]
    draft = q_ref.shape[0]
    vocab = q_ref.shape[2]
    shard = vocab // n_src
    seqs = q_ref.shape[1]
    n_out = acc_ref.shape[1]
    stride = draft + 1
    lane = lax.broadcasted_iota(jnp.int32, (seqs, LANE), 1)
    row = lax.broadcasted_iota(jnp.int32, (seqs, LANE), 0)
    tail = shard - (n_lt - 1) * LANE

    def tile(j, s, c):
        return z_ref[s, c, 0, pl.ds(j, seqs, stride=stride), :]

    wide = lax.broadcasted_iota(jnp.int32, (seqs, n_out), 1)
    deep = lax.broadcasted_iota(jnp.int32, (seqs, n_out), 0)
    accepts = []
    for j in range(stride):
        peak = None
        for s in range(n_src):
            for c in range(n_lt):
                z = tile(j, s, c)
                if c == n_lt - 1 and tail < LANE:
                    z = jnp.where(lane < tail, z, -jnp.inf)
                peak = z if peak is None else jnp.maximum(peak, z)
        peak = jnp.broadcast_to(jnp.max(peak, axis=1, keepdims=True), (seqs, LANE))
        out = (lambda g, v, j=j: res_ref.__setitem__((j, slice(None), slice(g * LANE, (g + 1) * LANE)), v)) if j < draft else (
            lambda g, v: bonus_ref.__setitem__((slice(None), slice(g * LANE, (g + 1) * LANE)), v))
        got = (lambda g, j=j: res_ref[j, :, g * LANE:(g + 1) * LANE]) if j < draft else (lambda g: bonus_ref[:, g * LANE:(g + 1) * LANE])
        total = jnp.zeros((seqs, LANE), jnp.float32)
        pend = None
        for s in range(n_src):
            off = s * shard % LANE
            base = s * shard // LANE
            for c in range(n_lt):
                e = jnp.exp(tile(j, s, c) - peak)
                if c == n_lt - 1 and tail < LANE:
                    e = jnp.where(lane < tail, e, 0.0)
                total = total + e
                r = pltpu.roll(e, off, 1) if off else e
                v = jnp.where(lane < off, pend, r) if off else r
                if c == n_lt - 1 and off + tail < LANE:
                    pend = v
                else:
                    out(base + c, v)
                    pend = r
        inv = jnp.broadcast_to(1.0 / jnp.sum(total, axis=1, keepdims=True), (seqs, LANE))
        n_g = vocab // LANE
        if j == draft:
            for g in range(n_g):
                out(g, got(g) * inv)
            continue
        excess = jnp.zeros((seqs, LANE), jnp.float32)
        for g in range(n_g):
            excess = excess + jnp.maximum(got(g) * inv - q_ref[j, :, g * LANE:(g + 1) * LANE], 0.0)
        p_pick = jnp.zeros((seqs, LANE), jnp.float32)
        q_pick = jnp.zeros((seqs, LANE), jnp.float32)
        for b in range(seqs):
            x = x_ref[(i * seqs + b) * draft + j]
            at = pl.multiple_of((x // LANE) * LANE, LANE)
            hit = (row == b) & (lane == x - at)
            p_pick = p_pick + jnp.where(hit, res_ref[j, :, pl.ds(at, LANE)], 0.0)
            q_pick = q_pick + jnp.where(hit, q_ref[j, :, pl.ds(at, LANE)], 0.0)
        p_col = jnp.sum(p_pick * inv, axis=1, keepdims=True)
        q_col = jnp.sum(q_pick, axis=1, keepdims=True)
        accepts.append(jnp.minimum(1.0, p_col / q_col))
        scale = jnp.broadcast_to(1.0 / jnp.sum(excess, axis=1, keepdims=True), (seqs, LANE))
        for g in range(n_g):
            out(g, jnp.maximum(got(g) * inv - q_ref[j, :, g * LANE:(g + 1) * LANE], 0.0) * scale)

    def to_lanes(col):
        return jnp.sum(jnp.where(wide == deep + i * seqs, jnp.broadcast_to(col, (seqs, n_out)), 0.0), axis=0, keepdims=True)

    @pl.when(i == 0)
    def _():
        acc_ref[...] = jnp.zeros_like(acc_ref)
        exp_ref[...] = jnp.zeros_like(exp_ref)

    run = None
    expected = None
    for j in range(draft):
        acc_ref[j:j + 1, :] += to_lanes(accepts[j])
        run = accepts[j] if j == 0 else run * accepts[j]
        expected = run if j == 0 else expected + run
    exp_ref[...] += to_lanes(expected)


def solution(mesh):
    n = mesh.shape["tp"]

    def local_step(hidden, w_shard, q_rows, x_group):
        seq_dev, draft, vocab = q_rows.shape
        batch, pos, depth = hidden.shape
        shard = w_shard.shape[1]
        n_tiles = pl.cdiv(shard, TILE)
        n_lt = n_tiles * TILE // LANE
        rows = batch * pos // HALVES
        seg = rows // n
        part = seq_dev // HALVES

        h = hidden.reshape(batch * pos, depth)
        recv = pl.pallas_call(
            logits_kernel,
            out_shape=jax.ShapeDtypeStruct((n, n_lt, HALVES, seg, LANE), jnp.float32),
            in_specs=[pl.BlockSpec(memory_space=pl.ANY)] * 2,
            out_specs=pl.BlockSpec(memory_space=pl.ANY),
            scratch_shapes=[
                pltpu.VMEM((HALVES, rows, depth), jnp.bfloat16),
                pltpu.VMEM((SLOTS, TILE, depth), jnp.bfloat16),
                pltpu.VMEM((n_tiles * HALVES, TILE // LANE, rows, LANE), jnp.float32),
                pltpu.SemaphoreType.DMA((HALVES,)),
                pltpu.SemaphoreType.DMA((SLOTS,)),
                pltpu.SemaphoreType.DMA((1,)),
                pltpu.SemaphoreType.DMA((7,)),
                pltpu.SemaphoreType.DMA((7,)),
            ],
            compiler_params=pltpu.CompilerParams(collective_id=0, has_side_effects=True, vmem_limit_bytes=60 * 1024 * 1024),
            cost_estimate=pl.CostEstimate(flops=2 * batch * pos * depth * shard, bytes_accessed=2 * shard * depth, transcendentals=0),
            name="logits_exchange",
        )(h, w_shard.T)

        x_own = lax.dynamic_slice_in_dim(x_group, lax.axis_index("tp") * seq_dev, seq_dev, axis=0).reshape(-1)
        seqs = 8
        grid = seq_dev // seqs
        per = part // seqs
        q_t = q_rows.transpose(1, 0, 2)
        res, bonus, acc, expd = pl.pallas_call(
            verify_kernel,
            grid_spec=pltpu.PrefetchScalarGridSpec(
                num_scalar_prefetch=1,
                grid=(grid,),
                in_specs=[
                    pl.BlockSpec((n, n_lt, 1, seqs * pos, LANE), lambda i, x: (0, 0, i // per, i % per, 0)),
                    pl.BlockSpec((draft, seqs, vocab), lambda i, x: (0, i, 0)),
                ],
                out_specs=[
                    pl.BlockSpec((draft, seqs, vocab), lambda i, x: (0, i, 0)),
                    pl.BlockSpec((seqs, vocab), lambda i, x: (i, 0)),
                    pl.BlockSpec((draft, seq_dev), lambda i, x: (0, 0)),
                    pl.BlockSpec((1, seq_dev), lambda i, x: (0, 0)),
                ],
            ),
            out_shape=[
                jax.ShapeDtypeStruct((draft, seq_dev, vocab), jnp.float32),
                jax.ShapeDtypeStruct((seq_dev, vocab), jnp.float32),
                jax.ShapeDtypeStruct((draft, seq_dev), jnp.float32),
                jax.ShapeDtypeStruct((1, seq_dev), jnp.float32),
            ],
            compiler_params=pltpu.CompilerParams(dimension_semantics=("arbitrary",), vmem_limit_bytes=60 * 1024 * 1024),
            name="verify_rows",
        )(x_own, recv, q_t)
        return acc.T, expd.reshape(seq_dev), res.transpose(1, 0, 2), bonus

    return jax.shard_map(local_step, mesh=mesh,
                         in_specs=(P("dp", None, None), P(None, "tp"), P(("dp", "tp"), None, None), P("dp", None)),
                         out_specs=(P(("dp", "tp"), None), P(("dp", "tp")), P(("dp", "tp"), None, None), P(("dp", "tp"), None)),
                         check_vma=False)
```

time: 416 us -> 238 us (0.57)
  Pallas kernels: 0 us -> 212 us
  waiting for transfers between devices: 181 us -> 0 us
  matrix products: 91.4 us -> 0 us
  local copies, waits for them, and re-layouts: 82.2 us -> 25.2 us
  other arithmetic: 55 us -> 0 us
  starting transfers between devices: 4.8 us -> 0 us
    pallas_call x0 -> x2, Pallas kernels: none -> 212 us  [the longest x1 192 us: local_step(): pl.pallas_call(logits_kernel, out_shape=jax.ShapeDtypeStruct((n, n_lt, HA...]
    all_to_all x1 -> x0, waiting for transfers between devices: 181 us -> none  [local_step(): seq_logits = lax.all_to_all(logits, 'tp', 0, 2, tiled=True)]
    dot_general x1 -> x0, matrix products: 91.4 us -> none  [local_step(): jnp.einsum('bjd,dv->bjv', hidden, w_shard, preferred_element_type=jnp.flo...]
    all_to_all x3 -> x0, local copies, waits for them, and re-layouts: 44.1 us -> none  [local_step(): seq_logits = lax.all_to_all(logits, 'tp', 0, 2, tiled=True)]
    div x2 -> x0, other arithmetic: 29.8 us -> none  [the longest x1 18 us: verify_rows(): residual = excess / jnp.sum(excess, axis=-1, keepdims=True)]
    reshape x0 -> x2, local copies, waits for them, and re-layouts: none -> 24.3 us  [the longest x1 23.6 us: local_step(): h = hidden.reshape(batch * pos, depth)]
    mul x1 -> x0, local copies, waits for them, and re-layouts: 20.2 us -> none  [local_step(): jnp.einsum('bjd,dv->bjv', hidden, w_shard, preferred_element_type=jnp.flo...]
    reduce_sum x3 -> x0, other arithmetic: 18.2 us -> none  [the longest x1 9.37 us: verify_rows(): residual = excess / jnp.sum(excess, axis=-1, keepdims=True)]
  transfers between devices with their start and end apart: 1 -> 0, of which waited for: 1 -> 0; matrix products, arithmetic and copies ran while one was open for 1% -> 0% of each run, Pallas kernels for 0% -> 0%
where the time goes in v1:
time: 238 us; the launch traced here: 237 us
  Pallas kernels  212 us (89%)
  local copies, waits for them, and re-layouts  25.2 us (11%)
    pallas_call x1, Pallas kernels, local_step(): pl.pallas_call(logits_kernel, out_shape=jax.ShapeDtypeStruct((n, n_lt, HA...  192 us
    reshape x1, local copies, waits for them, and re-layouts, local_step(): h = hidden.reshape(batch * pos, depth)  23.6 us
    pallas_call x1, Pallas kernels, local_step(): pl.pallas_call(verify_kernel, grid_spec=pltpu.PrefetchScalarGridSpec(num_...  19.6 us

profile of v1, /device:TPU:0, one launch (start us, length us, event | category | flops | bytes accessed | tf_op | source)
XLA Modules:
  0.0 237.5 jit_solution(5626460284737252207)
XLA Ops:
  0.6 0.0 copy-start
  0.7 0.7 copy-done
  1.3 0.1 constant_dynamic-slice_fusion
  1.4 0.1 copy.9
  1.5 0.7 reshape.17.x_ref
  2.2 23.6 %reshape.18.h_ref = bf16[1024,8192]{1,0:T(8,128)(2,1)} reshape(bf16[256,4,8192]{2,1,0:T(4,128)(2,1)} %param.4) | data formatting | bytes 33554432 | tf_op jit(solution)/shard_map/reshape | solution.py:236
  25.8 0.0 copy-start.1
  25.8 192.1 %logits_exchange.1.z_ref = f32[8,32,2,64,128]{4,3,2,1,0:T(8,128)} custom-call(bf16[1024,8192]{1,0:T(8,128)(2,1)} %reshape.18.h_ref, bf16[4000,8192]{1,0:T(8,128)(2,1)} %bitcast.6), custom_call_target="tpu_custom_call" | custom-call | flops 67108864000 | bytes 65536000 | tf_op jit(solution)/shard_map/logits_exchange/pallas_call | solution.py:237
  217.9 19.6 %verify_rows.1 = (f32[3,32,32000]{2,1,0:T(8,128)}, f32[32,32000]{1,0:T(8,128)}, f32[3,32]{1,0:T(4,128)}, f32[1,32]{1,0:T(1,128)}) custom-call(s32[96]{0:T(128)} %reshape.17.x_ref, f32[8,32,2,64,128]{4,3,2,1,0:T(8,128)} %logits_exchange.1.z_ref, f32[3,32,32000]{2,1,0:T(8,128)} %bitcast.5), custom_call_target="tpu_custom_call" | custom-call | tf_op jit(solution)/shard_map/verify_rows/pallas_call | solution.py:262
  237.5 0.0 copy-done.1
Async XLA Ops:
  0.6 0.7 copy-start
  25.8 211.7 %copy-start.1 = (s32[256,3]{0,1:T(4,128)S(1)}, s32[256,3]{0,1:T(4,128)}, u32[]{:S(2)}) copy-start(s32[256,3]{0,1:T(4,128)} %param.7) | copy-start | bytes 9220

commit v2 on v1

--- a/solution.py
+++ b/solution.py
@@ -11,7 +11,7 @@
 MESH = pl.DeviceIdType.MESH
 LANE = 128
 TILE = 256
-HALVES = 2
+SEQS = 8
 SLOTS = 3
 ORDER = (6, 2, 4, 7, 3, 5, 1)
 
@@ -24,116 +24,165 @@
     return d
 
 
-def logits_kernel(h_ref, w_ref, recv_ref, h_buf, w_buf, send_buf, h_sem, w_sem, own_sem, send_sem, recv_sem):
+def logits_kernel(h_ref, w_ref, recv_ref, edge_ref, stage, h_buf, w_buf, send_buf, edge_buf, h_sem, w_sem, own_sem, send_sem, recv_sem,
+                  edge_send, edge_recv):
     me = lax.axis_index("tp")
-    vocab = w_ref.shape[0]
-    rows = h_buf.shape[1]
-    seg = rows // 8
+    vocab, depth = w_ref.shape
+    n_dev = recv_ref.shape[1]
+    groups = recv_ref.shape[0]
+    seqs = stage.shape[0] // n_dev
+    pos = stage.shape[1]
+    seg = seqs * pos
+    per_dev = groups * seqs
     n_tiles = pl.cdiv(vocab, TILE)
     last = vocab - (n_tiles - 1) * TILE
     lt = TILE // LANE
-
-    def w_copy(t, size):
-        slot = lax.rem(t, SLOTS)
+    full = vocab // LANE
+    tail = vocab - full * LANE
+    n_steps = groups * n_tiles
+    lane = lax.broadcasted_iota(jnp.int32, (seqs, LANE), 1)
+
+    def w_copy(u, size):
+        slot = lax.rem(u, SLOTS)
+        t = lax.rem(u, n_tiles)
         return pltpu.make_async_copy(w_ref.at[pl.ds(pl.multiple_of(t * TILE, TILE), size)], w_buf.at[slot, pl.ds(0, size)], w_sem.at[slot])
 
-    def w_start(t):
+    def on_tile(u, act):
+        t = lax.rem(u, n_tiles)
+
         @pl.when(t < n_tiles - 1)
         def _():
-            w_copy(t, TILE).start()
+            act(w_copy(u, TILE))
 
         @pl.when(t == n_tiles - 1)
         def _():
-            w_copy(t, last).start()
-
-    def w_wait(t):
-        @pl.when(t < n_tiles - 1)
-        def _():
-            w_copy(t, TILE).wait()
-
-        @pl.when(t == n_tiles - 1)
-        def _():
-            w_copy(t, last).wait()
-
-    def h_start(half):
-        for d in range(8):
-            src = h_ref.at[pl.ds((d * HALVES + half) * seg, seg)]
-            pltpu.make_async_copy(src, h_buf.at[half, pl.ds(d * seg, seg)], h_sem.at[half]).start()
-
-    def h_wait(half):
-        pltpu.make_async_copy(h_ref.at[pl.ds(0, rows)], h_buf.at[half], h_sem.at[half]).wait()
+            act(w_copy(u, last))
+
+    def h_copy(g, d):
+        src = h_ref.at[pl.ds(d * per_dev + g * seqs, seqs)]
+        return pltpu.make_async_copy(src, stage.at[pl.ds(d * seqs, seqs)], h_sem.at[d])
+
+    def h_start(g):
+        for d in range(n_dev):
+            h_copy(g, d).start()
+
+    def relayout(g):
+        for d in range(n_dev):
+            h_copy(g, d).wait()
+
+            def cols(c, carry):
+                at = pl.ds(pl.multiple_of(c * LANE, LANE), LANE)
+                h_buf[pl.ds(d * seg, seg), at] = stage[pl.ds(d * seqs, seqs), :, at].reshape(seg, LANE)
+                return carry
+
+            lax.fori_loop(0, depth // LANE, cols, 0, unroll=8)
 
     h_start(0)
     w_copy(0, TILE).start()
+    w_copy(1, TILE).start()
+
+    barrier = pltpu.get_barrier_semaphore()
+    for k in range(1, n_dev):
+        pl.semaphore_signal(barrier, inc=1, device_id={"tp": peer_of(me, k)}, device_id_type=MESH)
+
+    relayout(0)
     h_start(1)
-    w_copy(1, TILE).start()
-
-    barrier = pltpu.get_barrier_semaphore()
-    for k in range(1, 8):
-        pl.semaphore_signal(barrier, inc=1, device_id={"tp": peer_of(me, k)}, device_id_type=MESH)
-    pl.semaphore_wait(barrier, 7)
-
-    def step(i, carry):
-        t = i // HALVES
-        half = lax.rem(i, HALVES)
-        slot = lax.rem(t, SLOTS)
-
-        @pl.when(half == 0)
-        def _():
-            w_wait(t)
-
-            @pl.when(t + 2 < n_tiles)
-            def _():
-                w_start(t + 2)
-
-        @pl.when(i == 0)
-        def _():
-            h_wait(0)
-
-        @pl.when(i == 1)
-        def _():
-            h_wait(1)
-
-        z = lax.dot_general(h_buf[half], w_buf[slot], (((1,), (1,)), ((), ())), preferred_element_type=jnp.float32) * INV_TEMP
-        for c in range(lt):
-            send_buf[i, c] = z[:, c * LANE:(c + 1) * LANE]
+    pl.semaphore_wait(barrier, n_dev - 1)
+
+    def send(u, g, t, width):
+        def rows(d):
+            return pl.ds(pl.multiple_of(d * seg, seg), seg)
+
+        dst = recv_ref.at[g, me, pl.ds(t * lt, width)]
         for k in ORDER:
             d = peer_of(me, k)
             pltpu.make_async_remote_copy(
-                src_ref=send_buf.at[i, :, pl.ds(pl.multiple_of(d * seg, seg), seg)],
-                dst_ref=recv_ref.at[me, pl.ds(t * lt, lt), half],
+                src_ref=send_buf.at[u, pl.ds(0, width), rows(d)],
+                dst_ref=dst,
                 send_sem=send_sem.at[k - 1],
                 recv_sem=recv_sem.at[k - 1],
                 device_id={"tp": d},
                 device_id_type=MESH,
             ).start()
-        pltpu.make_async_copy(
-            send_buf.at[i, :, pl.ds(pl.multiple_of(me * seg, seg), seg)],
-            recv_ref.at[me, pl.ds(t * lt, lt), half],
-            own_sem.at[0],
-        ).start()
+        pltpu.make_async_copy(send_buf.at[u, pl.ds(0, width), rows(me)], dst, own_sem.at[0]).start()
+
+    def send_edge(u, g):
+        for d in range(n_dev):
+            packed = jnp.zeros((seqs, LANE), jnp.float32)
+            for j in range(pos):
+                v = send_buf[u, 1, pl.ds(d * seg + j, seqs, stride=pos), :]
+                v = pltpu.roll(v, j * tail, 1) if j else v
+                packed = jnp.where((lane >= j * tail) & (lane < (j + 1) * tail), v, packed)
+            edge_buf[g, d] = packed
+        for k in ORDER:
+            d = peer_of(me, k)
+            pltpu.make_async_remote_copy(
+                src_ref=edge_buf.at[g, d],
+                dst_ref=edge_ref.at[g, me],
+                send_sem=edge_send.at[k - 1],
+                recv_sem=edge_recv.at[k - 1],
+                device_id={"tp": d},
+                device_id_type=MESH,
+            ).start()
+        pltpu.make_async_copy(edge_buf.at[g, me], edge_ref.at[g, me], own_sem.at[1]).start()
+
+    def step(u, carry):
+        g = u // n_tiles
+        t = lax.rem(u, n_tiles)
+        slot = lax.rem(u, SLOTS)
+
+        @pl.when((t == 0) & (g > 0))
+        def _():
+            relayout(g)
+
+            @pl.when(g + 1 < groups)
+            def _():
+                h_start(g + 1)
+
+        on_tile(u, lambda c: c.wait())
+
+        @pl.when(u + 2 < n_steps)
+        def _():
+            on_tile(u + 2, lambda c: c.start())
+
+        z = lax.dot_general(h_buf[...], w_buf[slot], (((1,), (1,)), ((), ())), preferred_element_type=jnp.float32) * INV_TEMP
+        for c in range(lt):
+            send_buf[u, c] = z[:, c * LANE:(c + 1) * LANE]
+
+        @pl.when(t < n_tiles - 1)
+        def _():
+            send(u, g, t, lt)
+
+        @pl.when(t == n_tiles - 1)
+        def _():
+            send(u, g, t, full - (n_tiles - 1) * lt)
+            send_edge(u, g)
+
         return carry
 
-    lax.fori_loop(0, n_tiles * HALVES, step, 0)
-
-    pltpu.make_async_copy(recv_ref.at[me], recv_ref.at[me], own_sem.at[0]).wait()
+    lax.fori_loop(0, n_steps, step, 0)
+
+    pltpu.make_async_copy(recv_ref.at[:, me], recv_ref.at[:, me], own_sem.at[0]).wait()
+    pltpu.make_async_copy(edge_ref.at[:, me], edge_ref.at[:, me], own_sem.at[1]).wait()
     for k in ORDER:
         d = peer_of(me, k)
-        done = pltpu.make_async_remote_copy(
-            src_ref=recv_ref.at[d],
-            dst_ref=recv_ref.at[d],
-            send_sem=send_sem.at[k - 1],
-            recv_sem=recv_sem.at[k - 1],
-            device_id={"tp": d},
-            device_id_type=MESH,
-        )
-        done.wait_send()
-        done.wait_recv()
-
-
-def verify_kernel(x_ref, z_ref, q_ref, res_ref, bonus_ref, acc_ref, exp_ref):
+        for ref, ss, rs in ((recv_ref, send_sem, recv_sem), (edge_ref, edge_send, edge_recv)):
+            done = pltpu.make_async_remote_copy(
+                src_ref=ref.at[:, d],
+                dst_ref=ref.at[:, d],
+                send_sem=ss.at[k - 1],
+                recv_sem=rs.at[k - 1],
+                device_id={"tp": d},
+                device_id_type=MESH,
+            )
+            done.wait_send()
+            done.wait_recv()
+
+
+def verify_kernel(x_ref, z_ref, edge_ref, q_ref, res_ref, bonus_ref, acc_ref, exp_ref):
     i = pl.program_id(0)
-    n_src, n_lt = z_ref.shape[0], z_ref.shape[1]
+    n_src, full = z_ref.shape[1], z_ref.shape[2]
+    n_lt = full + 1
     draft = q_ref.shape[0]
     vocab = q_ref.shape[2]
     shard = vocab // n_src
@@ -142,10 +191,13 @@
     stride = draft + 1
     lane = lax.broadcasted_iota(jnp.int32, (seqs, LANE), 1)
     row = lax.broadcasted_iota(jnp.int32, (seqs, LANE), 0)
-    tail = shard - (n_lt - 1) * LANE
+    tail = shard - full * LANE
 
     def tile(j, s, c):
-        return z_ref[s, c, 0, pl.ds(j, seqs, stride=stride), :]
+        if c < full:
+            return z_ref[0, s, c, pl.ds(j, seqs, stride=stride), :]
+        v = edge_ref[0, s]
+        return pltpu.roll(v, LANE - j * tail, 1) if j else v
 
     wide = lax.broadcasted_iota(jnp.int32, (seqs, n_out), 1)
     deep = lax.broadcasted_iota(jnp.int32, (seqs, n_out), 0)
@@ -228,44 +280,47 @@
         batch, pos, depth = hidden.shape
         shard = w_shard.shape[1]
         n_tiles = pl.cdiv(shard, TILE)
-        n_lt = n_tiles * TILE // LANE
-        rows = batch * pos // HALVES
-        seg = rows // n
-        part = seq_dev // HALVES
-
-        h = hidden.reshape(batch * pos, depth)
-        recv = pl.pallas_call(
+        groups = seq_dev // SEQS
+        rows = n * SEQS * pos
+        full = shard // LANE
+        recv, edge = pl.pallas_call(
             logits_kernel,
-            out_shape=jax.ShapeDtypeStruct((n, n_lt, HALVES, seg, LANE), jnp.float32),
+            out_shape=[
+                jax.ShapeDtypeStruct((groups, n, full, SEQS * pos, LANE), jnp.float32),
+                jax.ShapeDtypeStruct((groups, n, SEQS, LANE), jnp.float32),
+            ],
             in_specs=[pl.BlockSpec(memory_space=pl.ANY)] * 2,
-            out_specs=pl.BlockSpec(memory_space=pl.ANY),
+            out_specs=[pl.BlockSpec(memory_space=pl.ANY)] * 2,
             scratch_shapes=[
-                pltpu.VMEM((HALVES, rows, depth), jnp.bfloat16),
+                pltpu.VMEM((n * SEQS, pos, depth), jnp.bfloat16),
+                pltpu.VMEM((rows, depth), jnp.bfloat16),
                 pltpu.VMEM((SLOTS, TILE, depth), jnp.bfloat16),
-                pltpu.VMEM((n_tiles * HALVES, TILE // LANE, rows, LANE), jnp.float32),
-                pltpu.SemaphoreType.DMA((HALVES,)),
+                pltpu.VMEM((groups * n_tiles, TILE // LANE, rows, LANE), jnp.float32),
+                pltpu.VMEM((groups, n, SEQS, LANE), jnp.float32),
+                pltpu.SemaphoreType.DMA((n,)),
                 pltpu.SemaphoreType.DMA((SLOTS,)),
-                pltpu.SemaphoreType.DMA((1,)),
-                pltpu.SemaphoreType.DMA((7,)),
-                pltpu.SemaphoreType.DMA((7,)),
+                pltpu.SemaphoreType.DMA((2,)),
+                pltpu.SemaphoreType.DMA((n - 1,)),
+                pltpu.SemaphoreType.DMA((n - 1,)),
+                pltpu.SemaphoreType.DMA((n - 1,)),
+                pltpu.SemaphoreType.DMA((n - 1,)),
             ],
             compiler_params=pltpu.CompilerParams(collective_id=0, has_side_effects=True, vmem_limit_bytes=60 * 1024 * 1024),
             cost_estimate=pl.CostEstimate(flops=2 * batch * pos * depth * shard, bytes_accessed=2 * shard * depth, transcendentals=0),
             name="logits_exchange",
-        )(h, w_shard.T)
+        )(hidden, w_shard.T)
 
         x_own = lax.dynamic_slice_in_dim(x_group, lax.axis_index("tp") * seq_dev, seq_dev, axis=0).reshape(-1)
-        seqs = 8
-        grid = seq_dev // seqs
-        per = part // seqs
+        seqs = SEQS
         q_t = q_rows.transpose(1, 0, 2)
         res, bonus, acc, expd = pl.pallas_call(
             verify_kernel,
             grid_spec=pltpu.PrefetchScalarGridSpec(
                 num_scalar_prefetch=1,
-                grid=(grid,),
+                grid=(groups,),
                 in_specs=[
-                    pl.BlockSpec((n, n_lt, 1, seqs * pos, LANE), lambda i, x: (0, 0, i // per, i % per, 0)),
+                    pl.BlockSpec((1, n, full, seqs * pos, LANE), lambda i, x: (i, 0, 0, 0, 0)),
+                    pl.BlockSpec((1, n, seqs, LANE), lambda i, x: (i, 0, 0, 0)),
                     pl.BlockSpec((draft, seqs, vocab), lambda i, x: (0, i, 0)),
                 ],
                 out_specs=[
@@ -283,7 +338,7 @@
             ],
             compiler_params=pltpu.CompilerParams(dimension_semantics=("arbitrary",), vmem_limit_bytes=60 * 1024 * 1024),
             name="verify_rows",
-        )(x_own, recv, q_t)
+        )(x_own, recv, edge, q_t)
         return acc.T, expd.reshape(seq_dev), res.transpose(1, 0, 2), bonus
 
     return jax.shard_map(local_step, mesh=mesh,

time: 238 us -> 208 us (0.87)
  local copies, waits for them, and re-layouts: 25.2 us -> 1.48 us
  Pallas kernels: 212 us -> 206 us
    reshape x1 -> x0, local copies, waits for them, and re-layouts: 23.6 us -> none  [local_step(): h = hidden.reshape(batch * pos, depth)]
    pallas_call x1, Pallas kernels: 192 us -> 186 us  [local_step(): pl.pallas_call(logits_kernel, out_shape=[jax.ShapeDtypeStruct((groups, n,...]
where the time goes in v2:
time: 208 us
  Pallas kernels  206 us (99%)
    pallas_call x1, Pallas kernels, local_step(): pl.pallas_call(logits_kernel, out_shape=[jax.ShapeDtypeStruct((groups, n,...  186 us
    pallas_call x1, Pallas kernels, local_step(): pl.pallas_call(verify_kernel, grid_spec=pltpu.PrefetchScalarGridSpec(num_...  19.8 us

profile of v2, /device:TPU:0, one launch (start us, length us, event | category | flops | bytes accessed | tf_op | source)
XLA Modules:
  0.0 208.3 jit_solution(6464217522699664937)
XLA Ops:
  0.6 0.0 copy-start
  0.7 0.7 copy-done
  1.3 0.1 constant_dynamic-slice_fusion
  1.4 0.1 copy.9
  1.5 0.6 reshape.14.x_ref
  2.1 0.0 copy-start.1
  2.1 186.3 %logits_exchange.1 = (f32[4,8,31,32,128]{4,3,2,1,0:T(8,128)}, f32[4,8,8,128]{3,2,1,0:T(8,128)}) custom-call(bf16[256,4,8192]{2,1,0:T(4,128)(2,1)} %h_ref.1, bf16[4000,8192]{1,0:T(8,128)(2,1)} %bitcast.6), custom_call_target="tpu_custom_call" | custom-call | flops 67108864000 | bytes 65536000 | tf_op jit(solution)/shard_map/logits_exchange/pallas_call | solution.py:286
  188.4 19.8 %verify_rows.1 = (f32[3,32,32000]{2,1,0:T(8,128)}, f32[32,32000]{1,0:T(8,128)}, f32[3,32]{1,0:T(4,128)}, f32[1,32]{1,0:T(1,128)}) custom-call(s32[96]{0:T(128)} %reshape.14.x_ref, f32[4,8,31,32,128]{4,3,2,1,0:T(8,128)} %get-tuple-element.10.z_ref, f32[4,8,8,128]{3,2,1,0:T(8,128)} %get-tuple-element.11.edge_ref, f32[3,32,32000]{2,1,0:T(8,128)} %bitcast.5), custom_call_target="tpu_custom_call" | custom-call | tf_op jit(solution)/shard_map/verify_rows/pallas_call | solution.py:316
  208.3 0.0 copy-done.1
Async XLA Ops:
  0.6 0.7 copy-start
  2.1 206.1 %copy-start.1 = (s32[256,3]{0,1:T(4,128)S(1)}, s32[256,3]{0,1:T(4,128)}, u32[]{:S(2)}) copy-start(s32[256,3]{0,1:T(4,128)} %param.7) | copy-start | bytes 9220

commit v3 on v0

v3 whole, which is shorter than its diff:
```python
import jax
import jax.numpy as jnp
from jax import lax
from jax.experimental import pallas as pl
from jax.experimental.pallas import tpu as pltpu
from jax.sharding import PartitionSpec as P

INV_TEMP = 1.25
MESH = pl.DeviceIdType.MESH
LANE = 128
TILE = 256
SEQS = 8
SLOTS = 3
ORDER = (6, 2, 4, 7, 3, 5, 1)
CHAINS = 4
UNROLL = 25
MIB = 1024 * 1024
VMEM_A = 32
VMEM_B = 32


def peer_of(me, k):
    d = me
    for bit in (1, 2, 4):
        if k & bit:
            d = d + bit * (1 - 2 * ((me // bit) % 2))
    return d


def lanes(g):
    return pl.ds(pl.multiple_of(g * LANE, LANE), LANE)


def chained(op, n, unroll, term, parts):
    def body(c, parts):
        return (*parts[1:], op(parts[0], term(c)))

    return lax.fori_loop(0, n, body, parts, unroll=unroll)


def across(op, reduce, parts, shape):
    v = parts[0]
    for p in parts[1:]:
        v = op(v, p)
    return jnp.broadcast_to(reduce(v, axis=1, keepdims=True), shape)


def softmax_rows(tile, edge, put, n_src, full, tail, seqs):
    shard = full * LANE + tail
    shape = (seqs, LANE)
    lane = lax.broadcasted_iota(jnp.int32, shape, 1)
    parts = (tile(0, 0),) * CHAINS
    for s in range(n_src):
        parts = chained(jnp.maximum, full, full, lambda c: tile(s, c), parts)
        parts = (*parts[1:], jnp.maximum(parts[0], jnp.where(lane < tail, edge(s), -jnp.inf)))
    peak = across(jnp.maximum, jnp.max, parts, shape)
    pend = tile(0, 0) * 0.0
    parts = (pend,) * CHAINS
    for s in range(n_src):
        off = s * shard % LANE
        base = s * shard // LANE

        def place(i, e, pend):
            r = pltpu.roll(e, off, 1) if off else e
            v = jnp.where(lane < off, pend, r) if off else r
            return r, v

        def body(c, carry):
            pend, *parts = carry
            e = jnp.exp(tile(s, c) - peak)
            r, v = place(base + c, e, pend)
            put(base + c, v)
            return (r, *parts[1:], parts[0] + e)

        pend, *parts = lax.fori_loop(0, full, body, (pend, *parts), unroll=full)
        e = jnp.where(lane < tail, jnp.exp(edge(s) - peak), 0.0)
        parts = [*parts[1:], parts[0] + e]
        _, pend = place(base + full, e, pend)
        if off + tail == LANE:
            put(base + full, pend)
    return 1.0 / across(jnp.add, jnp.sum, parts, shape)


def finish_bonus(get, put, inv, n_g):
    def body(i, carry):
        put(i, get(i) * inv)
        return carry

    lax.fori_loop(0, n_g, body, 0, unroll=UNROLL)


def excess_rows(get, q_tile, inv, n_g):
    shape = inv.shape
    parts = chained(jnp.add, n_g, UNROLL, lambda i: jnp.maximum(get(i) * inv - q_tile(i), 0.0), (get(0) * 0.0,) * CHAINS)
    return 1.0 / across(jnp.add, jnp.sum, parts, shape)


def excess_rows_with_picks(get, q_tile, token, inv, n_g):
    shape = inv.shape
    lane = lax.broadcasted_iota(jnp.int32, shape, 1)
    row = lax.broadcasted_iota(jnp.int32, shape, 0)
    x = jnp.zeros(shape, jnp.int32)
    for b in range(shape[0]):
        x = jnp.where(row == b, token(b), x)
    x = x - lane

    def body(i, carry):
        p_pick, q_pick, *parts = carry
        p, q = get(i) * inv, q_tile(i)
        hit = x == i * LANE
        return (jnp.where(hit, p, p_pick), jnp.where(hit, q, q_pick), *parts[1:], parts[0] + jnp.maximum(p - q, 0.0))

    zero = get(0) * 0.0
    p_pick, q_pick, *parts = lax.fori_loop(0, n_g, body, (zero,) * (CHAINS + 2), unroll=UNROLL)
    return 1.0 / across(jnp.add, jnp.sum, parts, shape), accept_column(p_pick, q_pick)


def accept_column(p_pick, q_pick):
    return jnp.minimum(1.0, jnp.sum(p_pick, axis=1, keepdims=True) / jnp.sum(q_pick, axis=1, keepdims=True))


def picks_at(get_at, q_at, token, inv):
    shape = inv.shape
    lane = lax.broadcasted_iota(jnp.int32, shape, 1)
    row = lax.broadcasted_iota(jnp.int32, shape, 0)
    p_pick = jnp.zeros(shape, jnp.float32)
    q_pick = jnp.zeros(shape, jnp.float32)
    for b in range(shape[0]):
        x = token(b)
        at = pl.multiple_of((x // LANE) * LANE, LANE)
        hit = (row == b) & (lane == x - at)
        p_pick = jnp.where(hit, get_at(at) * inv, p_pick)
        q_pick = jnp.where(hit, q_at(at), q_pick)
    return accept_column(p_pick, q_pick)


def residual_rows(get, put, q_tile, inv, scale, n_g):
    def body(i, carry):
        put(i, jnp.maximum(get(i) * inv - q_tile(i), 0.0) * scale)
        return carry

    lax.fori_loop(0, n_g, body, 0, unroll=UNROLL)


def to_lanes(col, first, n_out):
    seqs = col.shape[0]
    wide = lax.broadcasted_iota(jnp.int32, (seqs, n_out), 1)
    deep = lax.broadcasted_iota(jnp.int32, (seqs, n_out), 0)
    return jnp.sum(jnp.where(wide == deep + first, jnp.broadcast_to(col, (seqs, n_out)), 0.0), axis=0, keepdims=True)


def prefixes(accepts):
    run, expected = accepts[0], accepts[0]
    for a in accepts[1:]:
        run = run * a
        expected = expected + run
    return expected


def exchange_kernel(x_ref, h_ref, w_ref, q_ref, recv_ref, edge_ref, done_ref, acc_ref, stage, h_buf, w_buf, z_buf, send_buf, edge_buf, q_buf,
                    h_sem, w_sem, q_sem, send_sem, recv_sem, edge_send, edge_recv):
    me = lax.axis_index("tp")
    vocab, depth = w_ref.shape
    groups, n_dev = recv_ref.shape[:2]
    seqs = stage.shape[0] // n_dev
    pos = stage.shape[1]
    draft = pos - 1
    seg = seqs * pos
    per_dev = groups * seqs
    n_tiles = pl.cdiv(vocab, TILE)
    last = vocab - (n_tiles - 1) * TILE
    lt = TILE // LANE
    full = vocab // LANE
    tail = vocab - full * LANE
    n_steps = groups * n_tiles
    lane = lax.broadcasted_iota(jnp.int32, (seqs, LANE), 1)

    def w_copy(u, size):
        slot = lax.rem(u, SLOTS)
        t = lax.rem(u, n_tiles)
        return pltpu.make_async_copy(w_ref.at[pl.ds(pl.multiple_of(t * TILE, TILE), size)], w_buf.at[slot, pl.ds(0, size)], w_sem.at[slot])

    def on_tile(u, act):
        t = lax.rem(u, n_tiles)

        @pl.when(t < n_tiles - 1)
        def _():
            act(w_copy(u, TILE))

        @pl.when(t == n_tiles - 1)
        def _():
            act(w_copy(u, last))

    def h_copy(g, d):
        src = h_ref.at[pl.ds(d * per_dev + g * seqs, seqs)]
        return pltpu.make_async_copy(src, stage.at[pl.ds(d * seqs, seqs)], h_sem.at[d])

    def h_start(g):
        for d in range(n_dev):
            h_copy(g, d).start()

    def relayout(g):
        for d in range(n_dev):
            h_copy(g, d).wait()

            def cols(c, carry):
                at = pl.ds(pl.multiple_of(c * LANE, LANE), LANE)
                h_buf[pl.ds(d * seg, seg), at] = stage[pl.ds(d * seqs, seqs), :, at].reshape(seg, LANE)
                return carry

            lax.fori_loop(0, depth // LANE, cols, 0, unroll=8)

    def q_copy(g, j):
        return pltpu.make_async_copy(q_ref.at[j, pl.ds(pl.multiple_of(g * seqs, seqs), seqs)], q_buf.at[j], q_sem.at[j])

    h_start(0)
    w_copy(0, TILE).start()
    w_copy(1, TILE).start()

    barrier = pltpu.get_barrier_semaphore()
    for k in range(1, n_dev):
        pl.semaphore_signal(barrier, inc=1, device_id={"tp": peer_of(me, k)}, device_id_type=MESH)

    acc_ref[...] = jnp.zeros_like(acc_ref)
    relayout(0)
    h_start(1)
    pl.semaphore_wait(barrier, n_dev - 1)

    def send(g, t, width):
        for c in range(width):
            recv_ref[g, me, t * lt + c] = send_buf[t, c, pl.ds(pl.multiple_of(me * seg, seg), seg), :]
        for k in ORDER:
            d = peer_of(me, k)
            pltpu.make_async_remote_copy(
                src_ref=send_buf.at[t, pl.ds(0, width), pl.ds(pl.multiple_of(d * seg, seg), seg)],
                dst_ref=recv_ref.at[g, me, pl.ds(t * lt, width)],
                send_sem=send_sem.at[t],
                recv_sem=recv_sem.at[g, k - 1],
                device_id={"tp": d},
                device_id_type=MESH,
            ).start()

    def wait_sent(t, width):
        ref = send_buf.at[t, pl.ds(0, width), pl.ds(0, (n_dev - 1) * seg)]
        pltpu.make_async_remote_copy(
            src_ref=ref, dst_ref=ref, send_sem=send_sem.at[t], recv_sem=recv_sem.at[0, 0],
            device_id={"tp": peer_of(me, 1)}, device_id_type=MESH,
        ).wait_send()

    def send_edge(g):
        for d in range(n_dev):
            packed = z_buf[1, pl.ds(d * seg, seqs, stride=pos), :]
            for j in range(1, pos):
                v = pltpu.roll(z_buf[1, pl.ds(d * seg + j, seqs, stride=pos), :], j * tail, 1)
                packed = jnp.where(lane < j * tail, packed, v)
            edge_buf[g, d] = packed
        edge_ref[g, me] = edge_buf[g, me]
        for k in ORDER:
            d = peer_of(me, k)
            pltpu.make_async_remote_copy(
                src_ref=edge_buf.at[g, d],
                dst_ref=edge_ref.at[g, me],
                send_sem=edge_send.at[k - 1],
                recv_sem=edge_recv.at[g, k - 1],
                device_id={"tp": d},
                device_id_type=MESH,
            ).start()

    rest = full - (n_tiles - 1) * lt

    def step(u, carry):
        g = u // n_tiles
        t = lax.rem(u, n_tiles)
        slot = lax.rem(u, SLOTS)

        @pl.when((t == 0) & (g > 0))
        def _():
            relayout(g)

            @pl.when(g + 1 < groups)
            def _():
                h_start(g + 1)

        on_tile(u, lambda c: c.wait())

        @pl.when(u + 2 < n_steps)
        def _():
            on_tile(u + 2, lambda c: c.start())

        z = lax.dot_general(h_buf[...], w_buf[slot], (((1,), (1,)), ((), ())), preferred_element_type=jnp.float32) * INV_TEMP
        for c in range(lt):
            z_buf[c] = z[:, c * LANE:(c + 1) * LANE]

        @pl.when((g > 0) & (t < n_tiles - 1))
        def _():
            wait_sent(t, lt)

        @pl.when((g > 0) & (t == n_tiles - 1))
        def _():
            wait_sent(t, rest)

        for c in range(lt):
            for d in range(n_dev):
                for j in range(pos):
                    send_buf[t, c, pl.ds(d * seg + j * seqs, seqs), :] = z_buf[c, pl.ds(d * seg + j, seqs, stride=pos), :]

        @pl.when(t < n_tiles - 1)
        def _():
            send(g, t, lt)

        @pl.when(t == n_tiles - 1)
        def _():
            send(g, t, rest)
            send_edge(g)

        return carry

    lax.fori_loop(0, n_steps, step, 0)

    def wait_group(g):
        for k in ORDER:
            d = peer_of(me, k)
            for ref, ss, rs in ((recv_ref, edge_send, recv_sem), (edge_ref, edge_send, edge_recv)):
                pltpu.make_async_remote_copy(
                    src_ref=ref.at[g, d], dst_ref=ref.at[g, d], send_sem=ss.at[k - 1], recv_sem=rs.at[g, k - 1],
                    device_id={"tp": d}, device_id_type=MESH,
                ).wait_recv()

    for j in range(draft):
        q_copy(0, j).start()

    def finish(g, carry):
        wait_group(g)
        accepts = []
        for j in range(pos):
            def tile(s, c):
                return recv_ref[g, s, c, pl.ds(j * seqs, seqs), :]

            def edge(s):
                v = edge_ref[g, s]
                return pltpu.roll(v, LANE - j * tail, 1) if j else v

            def put(i, v):
                done_ref[g, j, :, lanes(i)] = v

            def get(i):
                return done_ref[g, j, :, lanes(i)]

            n_g = done_ref.shape[3] // LANE
            inv = softmax_rows(tile, edge, put, n_dev, full, tail, seqs)
            if j == draft:
                finish_bonus(get, put, inv, n_g)
                continue
            q_copy(g, j).wait()
            def q_tile(i):
                return q_buf[j, :, lanes(i)]

            scale, accept = excess_rows_with_picks(get, q_tile, lambda b: x_ref[j, me * per_dev + g * seqs + b], inv, n_g)
            accepts.append(accept)
            residual_rows(get, put, q_tile, inv, scale, n_g)

            @pl.when(g + 2 < groups)
            def _():
                q_copy(g + 1, j).start()

        for j in range(draft):
            acc_ref[j:j + 1, :] += to_lanes(accepts[j], g * seqs, per_dev)
        acc_ref[draft:pos, :] += to_lanes(prefixes(accepts), g * seqs, per_dev)
        return carry

    lax.fori_loop(0, groups - 1, finish, 0)
    wait_group(groups - 1)

    for t in range(n_tiles):
        wait_sent(t, lt if t < n_tiles - 1 else rest)
    for k in ORDER:
        d = peer_of(me, k)
        ref = edge_ref.at[:, d]
        pltpu.make_async_remote_copy(
            src_ref=ref, dst_ref=ref, send_sem=edge_send.at[k - 1], recv_sem=edge_recv.at[0, k - 1],
            device_id={"tp": d}, device_id_type=MESH,
        ).wait_send()


def output_kernel(x_ref, recv_ref, edge_ref, done_ref, part_ref, q_ref, res_ref, bonus_ref, acc_ref, exp_ref, row_buf, q_buf, q_sem, out_sem):
    me = lax.axis_index("tp")
    groups, n_dev, full = recv_ref.shape[:3]
    seqs = edge_ref.shape[2]
    pos = done_ref.shape[1]
    draft = pos - 1
    vocab = done_ref.shape[3]
    n_g = vocab // LANE
    tail = vocab // n_dev - full * LANE
    per_dev = groups * seqs
    g_last = groups - 1

    def q_copy(j):
        return pltpu.make_async_copy(q_ref.at[j, pl.ds(g_last * seqs, seqs)], q_buf.at[j], q_sem.at[j])

    def out(g, j, src):
        dst = bonus_ref if j == draft else res_ref.at[j]
        return pltpu.make_async_copy(src, dst.at[pl.ds(g * seqs, seqs)], out_sem.at[g, j])

    for j in range(draft):
        q_copy(j).start()
    for g in range(g_last):
        for j in range(pos):
            out(g, j, done_ref.at[g, j]).start()

    accepts = []
    for j in (draft, *range(draft)):
        def tile(s, c):
            return recv_ref[g_last, s, c, pl.ds(j * seqs, seqs), :]

        def edge(s):
            v = edge_ref[g_last, s]
            return pltpu.roll(v, LANE - j * tail, 1) if j else v

        def put(i, v):
            row_buf[j, :, lanes(i)] = v

        def get(i):
            return row_buf[j, :, lanes(i)]

        inv = softmax_rows(tile, edge, put, n_dev, full, tail, seqs)
        if j == draft:
            finish_bonus(get, put, inv, n_g)
        else:
            q_copy(j).wait()
            def q_tile(i):
                return q_buf[j, :, lanes(i)]

            accepts.append(picks_at(
                lambda at: row_buf[j, :, pl.ds(at, LANE)], lambda at: q_buf[j, :, pl.ds(at, LANE)],
                lambda b: x_ref[j, me * per_dev + g_last * seqs + b], inv))
            residual_rows(get, put, q_tile, inv, excess_rows(get, q_tile, inv, n_g), n_g)
        out(g_last, j, row_buf.at[j]).start()

    for j in range(draft):
        acc_ref[j:j + 1, :] = part_ref[j:j + 1, :] + to_lanes(accepts[j], g_last * seqs, per_dev)
    exp_ref[...] = part_ref[draft:pos, :] + to_lanes(prefixes(accepts), g_last * seqs, per_dev)
    for g in range(groups):
        for j in range(pos):
            out(g, j, row_buf.at[j]).wait()


def solution(mesh):
    n = mesh.shape["tp"]

    def local_step(hidden, w_shard, q_rows, x_group):
        seq_dev, draft, vocab = q_rows.shape
        batch, pos, depth = hidden.shape
        shard = w_shard.shape[1]
        n_tiles = pl.cdiv(shard, TILE)
        groups = seq_dev // SEQS
        rows = n * SEQS * pos
        full = shard // LANE
        dma = pltpu.SemaphoreType.DMA
        in_hbm = pl.BlockSpec(memory_space=pltpu.HBM)
        in_vmem = pl.BlockSpec(memory_space=pltpu.VMEM)
        in_smem = pl.BlockSpec(memory_space=pltpu.SMEM)
        x_t = x_group.T
        q_hbm = pltpu.with_memory_space_constraint(q_rows.transpose(1, 0, 2), pltpu.HBM)

        recv, edge, done, part = pl.pallas_call(
            exchange_kernel,
            out_shape=[
                pltpu.VMEM((groups, n, full, SEQS * pos, LANE), jnp.float32),
                pltpu.VMEM((groups, n, SEQS, LANE), jnp.float32),
                pltpu.VMEM((groups - 1, pos, SEQS, vocab), jnp.float32),
                pltpu.VMEM((pos, seq_dev), jnp.float32),
            ],
            in_specs=[in_smem, in_hbm, in_hbm, in_hbm],
            out_specs=[in_vmem] * 4,
            scratch_shapes=[
                pltpu.VMEM((n * SEQS, pos, depth), jnp.bfloat16),
                pltpu.VMEM((rows, depth), jnp.bfloat16),
                pltpu.VMEM((SLOTS, TILE, depth), jnp.bfloat16),
                pltpu.VMEM((TILE // LANE, rows, LANE), jnp.float32),
                pltpu.VMEM((n_tiles, TILE // LANE, rows, LANE), jnp.float32),
                pltpu.VMEM((groups, n, SEQS, LANE), jnp.float32),
                pltpu.VMEM((draft, SEQS, vocab), jnp.float32),
                dma((n,)),
                dma((SLOTS,)),
                dma((draft,)),
                dma((n_tiles,)),
                dma((groups, n - 1)),
                dma((n - 1,)),
                dma((groups, n - 1)),
            ],
            compiler_params=pltpu.CompilerParams(collective_id=0, has_side_effects=True, vmem_limit_bytes=VMEM_A * MIB),
            cost_estimate=pl.CostEstimate(flops=2 * batch * pos * depth * shard, bytes_accessed=2 * shard * depth, transcendentals=0),
            name="logits_exchange",
        )(x_t, hidden, w_shard.T, q_hbm)

        res, bonus, acc, expd = pl.pallas_call(
            output_kernel,
            out_shape=[
                jax.ShapeDtypeStruct((draft, seq_dev, vocab), jnp.float32),
                jax.ShapeDtypeStruct((seq_dev, vocab), jnp.float32),
                jax.ShapeDtypeStruct((draft, seq_dev), jnp.float32),
                jax.ShapeDtypeStruct((1, seq_dev), jnp.float32),
            ],
            in_specs=[in_smem, in_vmem, in_vmem, in_vmem, in_vmem, in_hbm],
            out_specs=[in_hbm, in_hbm, in_vmem, in_vmem],
            scratch_shapes=[
                pltpu.VMEM((pos, SEQS, vocab), jnp.float32),
                pltpu.VMEM((draft, SEQS, vocab), jnp.float32),
                dma((draft,)),
                dma((groups, pos)),
            ],
            compiler_params=pltpu.CompilerParams(vmem_limit_bytes=VMEM_B * MIB),
            name="write_outputs",
        )(x_t, *(pltpu.with_memory_space_constraint(a, pltpu.VMEM) for a in (recv, edge, done, part)), q_hbm)
        return acc.T, expd.reshape(seq_dev), res.transpose(1, 0, 2), bonus

    return jax.shard_map(local_step, mesh=mesh,
                         in_specs=(P("dp", None, None), P(None, "tp"), P(("dp", "tp"), None, None), P("dp", None)),
                         out_specs=(P(("dp", "tp"), None), P(("dp", "tp")), P(("dp", "tp"), None, None), P(("dp", "tp"), None)),
                         check_vma=False)
```

time: 416 us -> 200 us (0.48)
  Pallas kernels: 0 us -> 199 us
  waiting for transfers between devices: 181 us -> 0 us
  matrix products: 91.4 us -> 0 us
  local copies, waits for them, and re-layouts: 82.2 us -> 0 us
  other arithmetic: 55 us -> 0 us
  starting transfers between devices: 4.8 us -> 0 us
    pallas_call x0 -> x2, Pallas kernels: none -> 199 us  [the longest x1 188 us: local_step(): pl.pallas_call(exchange_kernel, out_shape=[pltpu.VMEM((groups, n, full, S...]
    all_to_all x1 -> x0, waiting for transfers between devices: 181 us -> none  [local_step(): seq_logits = lax.all_to_all(logits, 'tp', 0, 2, tiled=True)]
    dot_general x1 -> x0, matrix products: 91.4 us -> none  [local_step(): jnp.einsum('bjd,dv->bjv', hidden, w_shard, preferred_element_type=jnp.flo...]
    all_to_all x3 -> x0, local copies, waits for them, and re-layouts: 44.1 us -> none  [local_step(): seq_logits = lax.all_to_all(logits, 'tp', 0, 2, tiled=True)]
    div x2 -> x0, other arithmetic: 29.8 us -> none  [the longest x1 18 us: verify_rows(): residual = excess / jnp.sum(excess, axis=-1, keepdims=True)]
    mul x1 -> x0, local copies, waits for them, and re-layouts: 20.2 us -> none  [local_step(): jnp.einsum('bjd,dv->bjv', hidden, w_shard, preferred_element_type=jnp.flo...]
    reduce_sum x3 -> x0, other arithmetic: 18.2 us -> none  [the longest x1 9.37 us: verify_rows(): residual = excess / jnp.sum(excess, axis=-1, keepdims=True)]
    gather x8 -> x0, local copies, waits for them, and re-layouts: 7.79 us -> none  [the longest x5 3.98 us: verify_rows(): p_pick = jnp.take_along_axis(draft_p, x_rows[:, :, None], axis=2)[:, :, 0]]
  transfers between devices with their start and end apart: 1 -> 0, of which waited for: 1 -> 0; matrix products, arithmetic and copies ran while one was open for 1% -> 0% of each run, Pallas kernels for 0% -> 0%
where the time goes in v3:
time: 200 us
  Pallas kernels  199 us (100%)
    pallas_call x1, Pallas kernels, local_step(): pl.pallas_call(exchange_kernel, out_shape=[pltpu.VMEM((groups, n, full, S...  188 us
    pallas_call x1, Pallas kernels, local_step(): pl.pallas_call(output_kernel, out_shape=[jax.ShapeDtypeStruct((draft, seq...  11.5 us

profile of v3, /device:TPU:0, one launch (start us, length us, event | category | flops | bytes accessed | tf_op | source)
XLA Modules:
  0.0 199.7 jit_solution(15354114581098747667)
XLA Ops:
  0.6 187.5 %logits_exchange.1 = (f32[4,8,31,32,128]{4,3,2,1,0:T(8,128)S(1)}, f32[4,8,8,128]{3,2,1,0:T(8,128)S(1)}, f32[3,4,8,32000]{3,2,1,0:T(8,128)S(1)}, f32[4,32]{1,0:T(4,128)S(1)}) custom-call(s32[3,256]{1,0:T(4,128)} %bitcast.8, bf16[256,4,8192]{2,1,0:T(4,128)(2,1)} %h_ref.1, bf16[4000,8192]{1,0:T(8,128)(2,1)} %bitcast.10, f32[3,32,32000]{2,1,0:T(8,128)} %bitcast.6), custom_call_target="tpu_custom_call" | custom-call | flops 67108864000 | bytes 65536000 | tf_op jit(solution)/shard_map/logits_exchange/pallas_call | solution.py:465
  188.2 11.5 %write_outputs.1 = (f32[3,32,32000]{2,1,0:T(8,128)}, f32[32,32000]{1,0:T(8,128)}, f32[3,32]{1,0:T(4,128)}, f32[1,32]{1,0:T(1,128)}) custom-call(s32[3,256]{1,0:T(4,128)} %bitcast.9, f32[4,8,31,32,128]{4,3,2,1,0:T(8,128)S(1)} %get-tuple-element.12.recv_ref, f32[4,8,8,128]{3,2,1,0:T(8,128)S(1)} %get-tuple-element.13.edge_ref, ...), custom_call_target="tpu_custom_call" | custom-call | tf_op jit(solution)/shard_map/write_outputs/pallas_call | solution.py:496

commit v4 on v3

--- a/solution.py
+++ b/solution.py
@@ -13,7 +13,7 @@
 SLOTS = 3
 ORDER = (6, 2, 4, 7, 3, 5, 1)
 CHAINS = 4
-UNROLL = 25
+WIDE = 25
 MIB = 1024 * 1024
 VMEM_A = 32
 VMEM_B = 32
@@ -31,6 +31,10 @@
     return pl.ds(pl.multiple_of(g * LANE, LANE), LANE)
 
 
+def chunk(i):
+    return pl.ds(pl.multiple_of(i * (WIDE * LANE), LANE), WIDE * LANE)
+
+
 def chained(op, n, unroll, term, parts):
     def body(c, parts):
         return (*parts[1:], op(parts[0], term(c)))
@@ -38,11 +42,11 @@
     return lax.fori_loop(0, n, body, parts, unroll=unroll)
 
 
-def across(op, reduce, parts, shape):
+def across(op, reduce, parts):
     v = parts[0]
     for p in parts[1:]:
         v = op(v, p)
-    return jnp.broadcast_to(reduce(v, axis=1, keepdims=True), shape)
+    return reduce(v, axis=1, keepdims=True)
 
 
 def softmax_rows(tile, edge, put, n_src, full, tail, seqs):
@@ -53,7 +57,7 @@
     for s in range(n_src):
         parts = chained(jnp.maximum, full, full, lambda c: tile(s, c), parts)
         parts = (*parts[1:], jnp.maximum(parts[0], jnp.where(lane < tail, edge(s), -jnp.inf)))
-    peak = across(jnp.maximum, jnp.max, parts, shape)
+    peak = jnp.broadcast_to(across(jnp.maximum, jnp.max, parts), shape)
     pend = tile(0, 0) * 0.0
     parts = (pend,) * CHAINS
     for s in range(n_src):
@@ -78,7 +82,13 @@
         _, pend = place(base + full, e, pend)
         if off + tail == LANE:
             put(base + full, pend)
-    return 1.0 / across(jnp.add, jnp.sum, parts, shape)
+    return 1.0 / across(jnp.add, jnp.sum, parts)
+
+
+def fold(op, parts, wide):
+    for k in range(0, wide.shape[1], LANE):
+        parts = (*parts[1:], op(parts[0], wide[:, k:k + LANE]))
+    return parts
 
 
 def finish_bonus(get, put, inv, n_g):
@@ -86,17 +96,18 @@
         put(i, get(i) * inv)
         return carry
 
-    lax.fori_loop(0, n_g, body, 0, unroll=UNROLL)
+    lax.fori_loop(0, n_g // WIDE, body, 0)
 
 
 def excess_rows(get, q_tile, inv, n_g):
-    shape = inv.shape
-    parts = chained(jnp.add, n_g, UNROLL, lambda i: jnp.maximum(get(i) * inv - q_tile(i), 0.0), (get(0) * 0.0,) * CHAINS)
-    return 1.0 / across(jnp.add, jnp.sum, parts, shape)
+    zero = get(0)[:, :LANE] * 0.0
+    parts = lax.fori_loop(
+        0, n_g // WIDE, lambda i, parts: fold(jnp.add, parts, jnp.maximum(get(i) * inv - q_tile(i), 0.0)), (zero,) * CHAINS)
+    return 1.0 / across(jnp.add, jnp.sum, parts)
 
 
 def excess_rows_with_picks(get, q_tile, token, inv, n_g):
-    shape = inv.shape
+    shape = (inv.shape[0], LANE)
     lane = lax.broadcasted_iota(jnp.int32, shape, 1)
     row = lax.broadcasted_iota(jnp.int32, shape, 0)
     x = jnp.zeros(shape, jnp.int32)
@@ -107,12 +118,15 @@
     def body(i, carry):
         p_pick, q_pick, *parts = carry
         p, q = get(i) * inv, q_tile(i)
-        hit = x == i * LANE
-        return (jnp.where(hit, p, p_pick), jnp.where(hit, q, q_pick), *parts[1:], parts[0] + jnp.maximum(p - q, 0.0))
-
-    zero = get(0) * 0.0
-    p_pick, q_pick, *parts = lax.fori_loop(0, n_g, body, (zero,) * (CHAINS + 2), unroll=UNROLL)
-    return 1.0 / across(jnp.add, jnp.sum, parts, shape), accept_column(p_pick, q_pick)
+        for k in range(WIDE):
+            hit = x == (i * WIDE + k) * LANE
+            p_pick = jnp.where(hit, p[:, k * LANE:(k + 1) * LANE], p_pick)
+            q_pick = jnp.where(hit, q[:, k * LANE:(k + 1) * LANE], q_pick)
+        return (p_pick, q_pick, *fold(jnp.add, tuple(parts), jnp.maximum(p - q, 0.0)))
+
+    zero = get(0)[:, :LANE] * 0.0
+    p_pick, q_pick, *parts = lax.fori_loop(0, n_g // WIDE, body, (zero,) * (CHAINS + 2))
+    return 1.0 / across(jnp.add, jnp.sum, parts), accept_column(p_pick, q_pick)
 
 
 def accept_column(p_pick, q_pick):
@@ -120,7 +134,7 @@
 
 
 def picks_at(get_at, q_at, token, inv):
-    shape = inv.shape
+    shape = (inv.shape[0], LANE)
     lane = lax.broadcasted_iota(jnp.int32, shape, 1)
     row = lax.broadcasted_iota(jnp.int32, shape, 0)
     p_pick = jnp.zeros(shape, jnp.float32)
@@ -139,7 +153,7 @@
         put(i, jnp.maximum(get(i) * inv - q_tile(i), 0.0) * scale)
         return carry
 
-    lax.fori_loop(0, n_g, body, 0, unroll=UNROLL)
+    lax.fori_loop(0, n_g // WIDE, body, 0)
 
 
 def to_lanes(col, first, n_out):
@@ -344,20 +358,23 @@
                 done_ref[g, j, :, lanes(i)] = v
 
             def get(i):
-                return done_ref[g, j, :, lanes(i)]
+                return done_ref[g, j, :, chunk(i)]
+
+            def put_wide(i, v):
+                done_ref[g, j, :, chunk(i)] = v
 
             n_g = done_ref.shape[3] // LANE
             inv = softmax_rows(tile, edge, put, n_dev, full, tail, seqs)
             if j == draft:
-                finish_bonus(get, put, inv, n_g)
+                finish_bonus(get, put_wide, inv, n_g)
                 continue
             q_copy(g, j).wait()
             def q_tile(i):
-                return q_buf[j, :, lanes(i)]
+                return q_buf[j, :, chunk(i)]
 
             scale, accept = excess_rows_with_picks(get, q_tile, lambda b: x_ref[j, me * per_dev + g * seqs + b], inv, n_g)
             accepts.append(accept)
-            residual_rows(get, put, q_tile, inv, scale, n_g)
+            residual_rows(get, put_wide, q_tile, inv, scale, n_g)
 
             @pl.when(g + 2 < groups)
             def _():
@@ -420,20 +437,23 @@
             row_buf[j, :, lanes(i)] = v
 
         def get(i):
-            return row_buf[j, :, lanes(i)]
+            return row_buf[j, :, chunk(i)]
+
+        def put_wide(i, v):
+            row_buf[j, :, chunk(i)] = v
 
         inv = softmax_rows(tile, edge, put, n_dev, full, tail, seqs)
         if j == draft:
-            finish_bonus(get, put, inv, n_g)
+            finish_bonus(get, put_wide, inv, n_g)
         else:
             q_copy(j).wait()
             def q_tile(i):
-                return q_buf[j, :, lanes(i)]
+                return q_buf[j, :, chunk(i)]
 
             accepts.append(picks_at(
                 lambda at: row_buf[j, :, pl.ds(at, LANE)], lambda at: q_buf[j, :, pl.ds(at, LANE)],
                 lambda b: x_ref[j, me * per_dev + g_last * seqs + b], inv))
-            residual_rows(get, put, q_tile, inv, excess_rows(get, q_tile, inv, n_g), n_g)
+            residual_rows(get, put_wide, q_tile, inv, excess_rows(get, q_tile, inv, n_g), n_g)
         out(g_last, j, row_buf.at[j]).start()
 
     for j in range(draft):

time: 200 us -> 196 us (0.980)
  Pallas kernels: 199 us -> 195 us
    pallas_call x1, Pallas kernels: 11.5 us -> 7.69 us  [local_step(): pl.pallas_call(output_kernel, out_shape=[jax.ShapeDtypeStruct((draft, seq...]
where the time goes in v4:
time: 196 us
  Pallas kernels  195 us (99%)
    pallas_call x1, Pallas kernels, local_step(): pl.pallas_call(exchange_kernel, out_shape=[pltpu.VMEM((groups, n, full, S...  188 us
    pallas_call x1, Pallas kernels, local_step(): pl.pallas_call(output_kernel, out_shape=[jax.ShapeDtypeStruct((draft, seq...  7.69 us

profile of v4, /device:TPU:0, one launch (start us, length us, event | category | flops | bytes accessed | tf_op | source)
XLA Modules:
  0.0 195.9 jit_solution(4256811890821131799)
XLA Ops:
  0.6 187.5 %logits_exchange.1 = (f32[4,8,31,32,128]{4,3,2,1,0:T(8,128)S(1)}, f32[4,8,8,128]{3,2,1,0:T(8,128)S(1)}, f32[3,4,8,32000]{3,2,1,0:T(8,128)S(1)}, f32[4,32]{1,0:T(4,128)S(1)}) custom-call(s32[3,256]{1,0:T(4,128)} %bitcast.8, bf16[256,4,8192]{2,1,0:T(4,128)(2,1)} %h_ref.1, bf16[4000,8192]{1,0:T(8,128)(2,1)} %bitcast.10, f32[3,32,32000]{2,1,0:T(8,128)} %bitcast.6), custom_call_target="tpu_custom_call" | custom-call | flops 67108864000 | bytes 65536000 | tf_op jit(solution)/shard_map/logits_exchange/pallas_call | solution.py:485
  188.2 7.7 %write_outputs.1 = (f32[3,32,32000]{2,1,0:T(8,128)}, f32[32,32000]{1,0:T(8,128)}, f32[3,32]{1,0:T(4,128)}, f32[1,32]{1,0:T(1,128)}) custom-call(s32[3,256]{1,0:T(4,128)} %bitcast.9, f32[4,8,31,32,128]{4,3,2,1,0:T(8,128)S(1)} %get-tuple-element.12.recv_ref, f32[4,8,8,128]{3,2,1,0:T(8,128)S(1)} %get-tuple-element.13.edge_ref, ...), custom_call_target="tpu_custom_call" | custom-call | tf_op jit(solution)/shard_map/write_outputs/pallas_call | solution.py:516

commit v5 on v4

--- a/solution.py
+++ b/solution.py
@@ -12,11 +12,12 @@
 SEQS = 8
 SLOTS = 3
 ORDER = (6, 2, 4, 7, 3, 5, 1)
+H_PART = 8
 CHAINS = 4
 WIDE = 25
 MIB = 1024 * 1024
-VMEM_A = 32
-VMEM_B = 32
+VMEM_A = 29
+VMEM_B = 29
 
 
 def peer_of(me, k):
@@ -171,13 +172,12 @@
     return expected
 
 
-def exchange_kernel(x_ref, h_ref, w_ref, q_ref, recv_ref, edge_ref, done_ref, acc_ref, stage, h_buf, w_buf, z_buf, send_buf, edge_buf, q_buf,
+def exchange_kernel(x_ref, h_ref, w_ref, q_ref, recv_ref, edge_ref, done_ref, acc_ref, q_buf, stage, h_buf, w_buf, z_buf, send_buf, edge_buf,
                     h_sem, w_sem, q_sem, send_sem, recv_sem, edge_send, edge_recv):
     me = lax.axis_index("tp")
     vocab, depth = w_ref.shape
     groups, n_dev = recv_ref.shape[:2]
-    seqs = stage.shape[0] // n_dev
-    pos = stage.shape[1]
+    seqs, pos = stage.shape[2:4]
     draft = pos - 1
     seg = seqs * pos
     per_dev = groups * seqs
@@ -205,24 +205,28 @@
         def _():
             act(w_copy(u, last))
 
-    def h_copy(g, d):
-        src = h_ref.at[pl.ds(d * per_dev + g * seqs, seqs)]
-        return pltpu.make_async_copy(src, stage.at[pl.ds(d * seqs, seqs)], h_sem.at[d])
+    def h_copy(g, c):
+        src = h_ref.at[:, pl.ds(pl.multiple_of(g * seqs, seqs), seqs), :, lanes(c)]
+        return pltpu.make_async_copy(src, stage.at[c], h_sem.at[c // H_PART])
 
     def h_start(g):
-        for d in range(n_dev):
-            h_copy(g, d).start()
+        for c in range(depth // LANE):
+            h_copy(g, c).start()
 
     def relayout(g):
-        for d in range(n_dev):
-            h_copy(g, d).wait()
+        flat = stage.reshape(depth // LANE, n_dev * seg, LANE)
+
+        def part(i, carry):
+            part_ref = stage.at[pl.ds(i * H_PART, H_PART)]
+            pltpu.make_async_copy(part_ref, part_ref, h_sem.at[i]).wait()
 
             def cols(c, carry):
-                at = pl.ds(pl.multiple_of(c * LANE, LANE), LANE)
-                h_buf[pl.ds(d * seg, seg), at] = stage[pl.ds(d * seqs, seqs), :, at].reshape(seg, LANE)
+                h_buf[:, lanes(i * H_PART + c)] = flat[i * H_PART + c]
                 return carry
 
-            lax.fori_loop(0, depth // LANE, cols, 0, unroll=8)
+            return lax.fori_loop(0, H_PART, cols, carry, unroll=True)
+
+        lax.fori_loop(0, depth // LANE // H_PART, part, 0)
 
     def q_copy(g, j):
         return pltpu.make_async_copy(q_ref.at[j, pl.ds(pl.multiple_of(g * seqs, seqs), seqs)], q_buf.at[j], q_sem.at[j])
@@ -376,9 +380,7 @@
             accepts.append(accept)
             residual_rows(get, put_wide, q_tile, inv, scale, n_g)
 
-            @pl.when(g + 2 < groups)
-            def _():
-                q_copy(g + 1, j).start()
+            q_copy(g + 1, j).start()
 
         for j in range(draft):
             acc_ref[j:j + 1, :] += to_lanes(accepts[j], g * seqs, per_dev)
@@ -386,6 +388,8 @@
         return carry
 
     lax.fori_loop(0, groups - 1, finish, 0)
+    for j in range(draft):
+        q_copy(groups - 1, j).wait()
     wait_group(groups - 1)
 
     for t in range(n_tiles):
@@ -399,7 +403,7 @@
         ).wait_send()
 
 
-def output_kernel(x_ref, recv_ref, edge_ref, done_ref, part_ref, q_ref, res_ref, bonus_ref, acc_ref, exp_ref, row_buf, q_buf, q_sem, out_sem):
+def output_kernel(x_ref, recv_ref, edge_ref, done_ref, part_ref, q_buf, res_ref, bonus_ref, acc_ref, exp_ref, row_buf, out_sem):
     me = lax.axis_index("tp")
     groups, n_dev, full = recv_ref.shape[:3]
     seqs = edge_ref.shape[2]
@@ -411,15 +415,10 @@
     per_dev = groups * seqs
     g_last = groups - 1
 
-    def q_copy(j):
-        return pltpu.make_async_copy(q_ref.at[j, pl.ds(g_last * seqs, seqs)], q_buf.at[j], q_sem.at[j])
-
     def out(g, j, src):
         dst = bonus_ref if j == draft else res_ref.at[j]
         return pltpu.make_async_copy(src, dst.at[pl.ds(g * seqs, seqs)], out_sem.at[g, j])
 
-    for j in range(draft):
-        q_copy(j).start()
     for g in range(g_last):
         for j in range(pos):
             out(g, j, done_ref.at[g, j]).start()
@@ -446,7 +445,6 @@
         if j == draft:
             finish_bonus(get, put_wide, inv, n_g)
         else:
-            q_copy(j).wait()
             def q_tile(i):
                 return q_buf[j, :, chunk(i)]
 
@@ -482,25 +480,25 @@
         x_t = x_group.T
         q_hbm = pltpu.with_memory_space_constraint(q_rows.transpose(1, 0, 2), pltpu.HBM)
 
-        recv, edge, done, part = pl.pallas_call(
+        recv, edge, done, part, q_last = pl.pallas_call(
             exchange_kernel,
             out_shape=[
                 pltpu.VMEM((groups, n, full, SEQS * pos, LANE), jnp.float32),
                 pltpu.VMEM((groups, n, SEQS, LANE), jnp.float32),
                 pltpu.VMEM((groups - 1, pos, SEQS, vocab), jnp.float32),
                 pltpu.VMEM((pos, seq_dev), jnp.float32),
+                pltpu.VMEM((draft, SEQS, vocab), jnp.float32),
             ],
             in_specs=[in_smem, in_hbm, in_hbm, in_hbm],
-            out_specs=[in_vmem] * 4,
+            out_specs=[in_vmem] * 5,
             scratch_shapes=[
-                pltpu.VMEM((n * SEQS, pos, depth), jnp.bfloat16),
+                pltpu.VMEM((depth // LANE, n, SEQS, pos, LANE), jnp.bfloat16),
                 pltpu.VMEM((rows, depth), jnp.bfloat16),
                 pltpu.VMEM((SLOTS, TILE, depth), jnp.bfloat16),
                 pltpu.VMEM((TILE // LANE, rows, LANE), jnp.float32),
                 pltpu.VMEM((n_tiles, TILE // LANE, rows, LANE), jnp.float32),
                 pltpu.VMEM((groups, n, SEQS, LANE), jnp.float32),
-                pltpu.VMEM((draft, SEQS, vocab), jnp.float32),
-                dma((n,)),
+                dma((depth // LANE // H_PART,)),
                 dma((SLOTS,)),
                 dma((draft,)),
                 dma((n_tiles,)),
@@ -511,7 +509,7 @@
             compiler_params=pltpu.CompilerParams(collective_id=0, has_side_effects=True, vmem_limit_bytes=VMEM_A * MIB),
             cost_estimate=pl.CostEstimate(flops=2 * batch * pos * depth * shard, bytes_accessed=2 * shard * depth, transcendentals=0),
             name="logits_exchange",
-        )(x_t, hidden, w_shard.T, q_hbm)
+        )(x_t, hidden.reshape(n, seq_dev, pos, depth), w_shard.T, q_hbm)
 
         res, bonus, acc, expd = pl.pallas_call(
             output_kernel,
@@ -521,17 +519,15 @@
                 jax.ShapeDtypeStruct((draft, seq_dev), jnp.float32),
                 jax.ShapeDtypeStruct((1, seq_dev), jnp.float32),
             ],
-            in_specs=[in_smem, in_vmem, in_vmem, in_vmem, in_vmem, in_hbm],
+            in_specs=[in_smem] + [in_vmem] * 5,
             out_specs=[in_hbm, in_hbm, in_vmem, in_vmem],
             scratch_shapes=[
                 pltpu.VMEM((pos, SEQS, vocab), jnp.float32),
-                pltpu.VMEM((draft, SEQS, vocab), jnp.float32),
-                dma((draft,)),
                 dma((groups, pos)),
             ],
             compiler_params=pltpu.CompilerParams(vmem_limit_bytes=VMEM_B * MIB),
             name="write_outputs",
-        )(x_t, *(pltpu.with_memory_space_constraint(a, pltpu.VMEM) for a in (recv, edge, done, part)), q_hbm)
+        )(x_t, *(pltpu.with_memory_space_constraint(a, pltpu.VMEM) for a in (recv, edge, done, part, q_last)))
         return acc.T, expd.reshape(seq_dev), res.transpose(1, 0, 2), bonus
 
     return jax.shard_map(local_step, mesh=mesh,

time: 196 us -> 195 us (level)
  no operation moved by 1% of the time
where the time goes in v5:
time: 195 us
  Pallas kernels  194 us (99%)
    pallas_call x1, Pallas kernels, local_step(): pl.pallas_call(exchange_kernel, out_shape=[pltpu.VMEM((groups, n, full, S...  187 us
    pallas_call x1, Pallas kernels, local_step(): pl.pallas_call(output_kernel, out_shape=[jax.ShapeDtypeStruct((draft, seq...  7.17 us

profile of v5, /device:TPU:0, one launch (start us, length us, event | category | flops | bytes accessed | tf_op | source)
XLA Modules:
  0.0 195.0 jit_solution(4003579762890413475)
XLA Ops:
  0.6 187.2 %logits_exchange.1 = (f32[4,8,31,32,128]{4,3,2,1,0:T(8,128)S(1)}, f32[4,8,8,128]{3,2,1,0:T(8,128)S(1)}, f32[3,4,8,32000]{3,2,1,0:T(8,128)S(1)}, f32[4,32]{1,0:T(4,128)S(1)}, f32[3,8,32000]{2,1,0:T(8,128)S(1)}) custom-call(s32[3,256]{1,0:T(4,128)} %bitcast.7, bf16[8,32,4,8192]{3,2,1,0:T(4,128)(2,1)} %bitcast.10, bf16[4000,8192]{1,0:T(8,128)(2,1)} %bitcast.9, ...), custom_call_target="tpu_custom_call" | custom-call | flops 67108864000 | bytes 65536000 | tf_op jit(solution)/shard_map/logits_exchange/pallas_call | solution.py:483
  187.9 7.2 %write_outputs.1 = (f32[3,32,32000]{2,1,0:T(8,128)}, f32[32,32000]{1,0:T(8,128)}, f32[3,32]{1,0:T(4,128)}, f32[1,32]{1,0:T(1,128)}) custom-call(s32[3,256]{1,0:T(4,128)} %bitcast.8, f32[4,8,31,32,128]{4,3,2,1,0:T(8,128)S(1)} %get-tuple-element.13.recv_ref, f32[4,8,8,128]{3,2,1,0:T(8,128)S(1)} %get-tuple-element.14.edge_ref, ...), custom_call_target="tpu_custom_call" | custom-call | tf_op jit(solution)/shard_map/write_outputs/pallas_call | solution.py:514

commit v6 on v5

--- a/solution.py
+++ b/solution.py
@@ -100,22 +100,16 @@
     lax.fori_loop(0, n_g // WIDE, body, 0)
 
 
-def excess_rows(get, q_tile, inv, n_g):
-    zero = get(0)[:, :LANE] * 0.0
-    parts = lax.fori_loop(
-        0, n_g // WIDE, lambda i, parts: fold(jnp.add, parts, jnp.maximum(get(i) * inv - q_tile(i), 0.0)), (zero,) * CHAINS)
-    return 1.0 / across(jnp.add, jnp.sum, parts)
-
-
-def excess_rows_with_picks(get, q_tile, token, inv, n_g):
-    shape = (inv.shape[0], LANE)
-    lane = lax.broadcasted_iota(jnp.int32, shape, 1)
+def token_tile(token, seqs):
+    shape = (seqs, LANE)
     row = lax.broadcasted_iota(jnp.int32, shape, 0)
     x = jnp.zeros(shape, jnp.int32)
-    for b in range(shape[0]):
+    for b in range(seqs):
         x = jnp.where(row == b, token(b), x)
-    x = x - lane
-
+    return x - lax.broadcasted_iota(jnp.int32, shape, 1)
+
+
+def excess_rows_with_picks(get, q_tile, x, inv, n_g):
     def body(i, carry):
         p_pick, q_pick, *parts = carry
         p, q = get(i) * inv, q_tile(i)
@@ -134,21 +128,6 @@
     return jnp.minimum(1.0, jnp.sum(p_pick, axis=1, keepdims=True) / jnp.sum(q_pick, axis=1, keepdims=True))
 
 
-def picks_at(get_at, q_at, token, inv):
-    shape = (inv.shape[0], LANE)
-    lane = lax.broadcasted_iota(jnp.int32, shape, 1)
-    row = lax.broadcasted_iota(jnp.int32, shape, 0)
-    p_pick = jnp.zeros(shape, jnp.float32)
-    q_pick = jnp.zeros(shape, jnp.float32)
-    for b in range(shape[0]):
-        x = token(b)
-        at = pl.multiple_of((x // LANE) * LANE, LANE)
-        hit = (row == b) & (lane == x - at)
-        p_pick = jnp.where(hit, get_at(at) * inv, p_pick)
-        q_pick = jnp.where(hit, q_at(at), q_pick)
-    return accept_column(p_pick, q_pick)
-
-
 def residual_rows(get, put, q_tile, inv, scale, n_g):
     def body(i, carry):
         put(i, jnp.maximum(get(i) * inv - q_tile(i), 0.0) * scale)
@@ -172,8 +151,8 @@
     return expected
 
 
-def exchange_kernel(x_ref, h_ref, w_ref, q_ref, recv_ref, edge_ref, done_ref, acc_ref, q_buf, stage, h_buf, w_buf, z_buf, send_buf, edge_buf,
-                    h_sem, w_sem, q_sem, send_sem, recv_sem, edge_send, edge_recv):
+def exchange_kernel(x_in, h_ref, w_ref, q_ref, recv_ref, edge_ref, done_ref, acc_ref, q_buf, token_ref, x_ref, stage, h_buf, w_buf, z_buf, send_buf, edge_buf,
+                    x_sem, h_sem, w_sem, q_sem, send_sem, recv_sem, edge_send, edge_recv):
     me = lax.axis_index("tp")
     vocab, depth = w_ref.shape
     groups, n_dev = recv_ref.shape[:2]
@@ -239,6 +218,7 @@
     for k in range(1, n_dev):
         pl.semaphore_signal(barrier, inc=1, device_id={"tp": peer_of(me, k)}, device_id_type=MESH)
 
+    pltpu.make_async_copy(x_in, x_ref, x_sem.at[0]).start()
     acc_ref[...] = jnp.zeros_like(acc_ref)
     relayout(0)
     h_start(1)
@@ -344,6 +324,7 @@
                     device_id={"tp": d}, device_id_type=MESH,
                 ).wait_recv()
 
+    pltpu.make_async_copy(x_in, x_ref, x_sem.at[0]).wait()
     for j in range(draft):
         q_copy(0, j).start()
 
@@ -376,7 +357,8 @@
             def q_tile(i):
                 return q_buf[j, :, chunk(i)]
 
-            scale, accept = excess_rows_with_picks(get, q_tile, lambda b: x_ref[j, me * per_dev + g * seqs + b], inv, n_g)
+            x = token_tile(lambda b: x_ref[j, me * per_dev + g * seqs + b], seqs)
+            scale, accept = excess_rows_with_picks(get, q_tile, x, inv, n_g)
             accepts.append(accept)
             residual_rows(get, put_wide, q_tile, inv, scale, n_g)
 
@@ -390,6 +372,7 @@
     lax.fori_loop(0, groups - 1, finish, 0)
     for j in range(draft):
         q_copy(groups - 1, j).wait()
+        token_ref[j] = token_tile(lambda b: x_ref[j, me * per_dev + (groups - 1) * seqs + b], seqs)
     wait_group(groups - 1)
 
     for t in range(n_tiles):
@@ -403,8 +386,8 @@
         ).wait_send()
 
 
-def output_kernel(x_ref, recv_ref, edge_ref, done_ref, part_ref, q_buf, res_ref, bonus_ref, acc_ref, exp_ref, row_buf, out_sem):
-    me = lax.axis_index("tp")
+def output_kernel(recv_ref, edge_ref, done_ref, part_ref, q_buf, token_ref, res_ref, bonus_ref, acc_ref, exp_ref, row_buf, acc_buf, exp_buf, out_sem,
+                  small_sem):
     groups, n_dev, full = recv_ref.shape[:3]
     seqs = edge_ref.shape[2]
     pos = done_ref.shape[1]
@@ -448,18 +431,22 @@
             def q_tile(i):
                 return q_buf[j, :, chunk(i)]
 
-            accepts.append(picks_at(
-                lambda at: row_buf[j, :, pl.ds(at, LANE)], lambda at: q_buf[j, :, pl.ds(at, LANE)],
-                lambda b: x_ref[j, me * per_dev + g_last * seqs + b], inv))
-            residual_rows(get, put_wide, q_tile, inv, excess_rows(get, q_tile, inv, n_g), n_g)
+            scale, accept = excess_rows_with_picks(get, q_tile, token_ref[j], inv, n_g)
+            accepts.append(accept)
+            residual_rows(get, put_wide, q_tile, inv, scale, n_g)
         out(g_last, j, row_buf.at[j]).start()
 
     for j in range(draft):
-        acc_ref[j:j + 1, :] = part_ref[j:j + 1, :] + to_lanes(accepts[j], g_last * seqs, per_dev)
-    exp_ref[...] = part_ref[draft:pos, :] + to_lanes(prefixes(accepts), g_last * seqs, per_dev)
+        acc_buf[j:j + 1, :] = part_ref[j:j + 1, :] + to_lanes(accepts[j], g_last * seqs, per_dev)
+    exp_buf[...] = part_ref[draft:pos, :] + to_lanes(prefixes(accepts), g_last * seqs, per_dev)
+    small = (pltpu.make_async_copy(acc_buf, acc_ref, small_sem.at[0]), pltpu.make_async_copy(exp_buf, exp_ref, small_sem.at[1]))
+    for c in small:
+        c.start()
     for g in range(groups):
         for j in range(pos):
             out(g, j, row_buf.at[j]).wait()
+    for c in small:
+        c.wait()
 
 
 def solution(mesh):
@@ -476,11 +463,10 @@
         dma = pltpu.SemaphoreType.DMA
         in_hbm = pl.BlockSpec(memory_space=pltpu.HBM)
         in_vmem = pl.BlockSpec(memory_space=pltpu.VMEM)
-        in_smem = pl.BlockSpec(memory_space=pltpu.SMEM)
         x_t = x_group.T
         q_hbm = pltpu.with_memory_space_constraint(q_rows.transpose(1, 0, 2), pltpu.HBM)
 
-        recv, edge, done, part, q_last = pl.pallas_call(
+        handed_on = pl.pallas_call(
             exchange_kernel,
             out_shape=[
                 pltpu.VMEM((groups, n, full, SEQS * pos, LANE), jnp.float32),
@@ -488,16 +474,19 @@
                 pltpu.VMEM((groups - 1, pos, SEQS, vocab), jnp.float32),
                 pltpu.VMEM((pos, seq_dev), jnp.float32),
                 pltpu.VMEM((draft, SEQS, vocab), jnp.float32),
+                pltpu.VMEM((draft, SEQS, LANE), jnp.int32),
             ],
-            in_specs=[in_smem, in_hbm, in_hbm, in_hbm],
-            out_specs=[in_vmem] * 5,
+            in_specs=[in_hbm] * 4,
+            out_specs=[in_vmem] * 6,
             scratch_shapes=[
+                pltpu.SMEM((draft, batch), jnp.int32),
                 pltpu.VMEM((depth // LANE, n, SEQS, pos, LANE), jnp.bfloat16),
                 pltpu.VMEM((rows, depth), jnp.bfloat16),
                 pltpu.VMEM((SLOTS, TILE, depth), jnp.bfloat16),
                 pltpu.VMEM((TILE // LANE, rows, LANE), jnp.float32),
                 pltpu.VMEM((n_tiles, TILE // LANE, rows, LANE), jnp.float32),
                 pltpu.VMEM((groups, n, SEQS, LANE), jnp.float32),
+                dma((1,)),
                 dma((depth // LANE // H_PART,)),
                 dma((SLOTS,)),
                 dma((draft,)),
@@ -519,15 +508,18 @@
                 jax.ShapeDtypeStruct((draft, seq_dev), jnp.float32),
                 jax.ShapeDtypeStruct((1, seq_dev), jnp.float32),
             ],
-            in_specs=[in_smem] + [in_vmem] * 5,
-            out_specs=[in_hbm, in_hbm, in_vmem, in_vmem],
+            in_specs=[in_vmem] * 6,
+            out_specs=[in_hbm] * 4,
             scratch_shapes=[
                 pltpu.VMEM((pos, SEQS, vocab), jnp.float32),
+                pltpu.VMEM((draft, seq_dev), jnp.float32),
+                pltpu.VMEM((1, seq_dev), jnp.float32),
                 dma((groups, pos)),
+                dma((2,)),
             ],
             compiler_params=pltpu.CompilerParams(vmem_limit_bytes=VMEM_B * MIB),
             name="write_outputs",
-        )(x_t, *(pltpu.with_memory_space_constraint(a, pltpu.VMEM) for a in (recv, edge, done, part, q_last)))
+        )(*(pltpu.with_memory_space_constraint(a, pltpu.VMEM) for a in handed_on))
         return acc.T, expd.reshape(seq_dev), res.transpose(1, 0, 2), bonus
 
     return jax.shard_map(local_step, mesh=mesh,

time: 195 us -> 193 us (0.990)
  Pallas kernels: 194 us -> 192 us
where the time goes in v6:
time: 193 us
  Pallas kernels  192 us (99%)
    pallas_call x1, Pallas kernels, local_step(): pl.pallas_call(exchange_kernel, out_shape=[pltpu.VMEM((groups, n, full, S...  187 us
    pallas_call x1, Pallas kernels, local_step(): pl.pallas_call(output_kernel, out_shape=[jax.ShapeDtypeStruct((draft, seq...  5.89 us

profile of v6, /device:TPU:0, one launch (start us, length us, event | category | flops | bytes accessed | tf_op | source)
XLA Modules:
  0.0 193.1 jit_solution(8570189365095091736)
XLA Ops:
  0.6 186.5 %logits_exchange.1 = (f32[4,8,31,32,128]{4,3,2,1,0:T(8,128)S(1)}, f32[4,8,8,128]{3,2,1,0:T(8,128)S(1)}, f32[3,4,8,32000]{3,2,1,0:T(8,128)S(1)}, f32[4,32]{1,0:T(...) custom-call(s32[3,256]{1,0:T(4,128)} %bitcast.11, bf16[8,32,4,8192]{3,2,1,0:T(4,128)(2,1)} %bitcast.8, ...), custom_call_target="tpu_custom_call" | custom-call | flops 67108864000 | bytes 65536000 | tf_op jit(solution)/shard_map/logits_exchange/pallas_call | solution.py:469
  187.2 5.9 %write_outputs.1 = (f32[3,32,32000]{2,1,0:T(8,128)}, f32[32,32000]{1,0:T(8,128)}, f32[3,32]{1,0:T(4,128)}, f32[1,32]{1,0:T(1,128)}) custom-call(f32[4,8,31,32,128]{4,3,2,1,0:T(8,128)S(1)} %get-tuple-element.14.recv_ref, f32[4,8,8,128]{3,2,1,0:T(8,128)S(1)} %get-tuple-element.15.edge_ref, f32[3,4,8,32000]{3,2,1,0:T(8,128)S(1)} %get-tuple-element.16.done_ref, ...), custom_call_target="tpu_custom_call" | custom-call | tf_op jit(solution)/shard_map/write_outputs/pallas_call | solution.py:503

commit v7 on v6

--- a/solution.py
+++ b/solution.py
@@ -152,7 +152,7 @@
 
 
 def exchange_kernel(x_in, h_ref, w_ref, q_ref, recv_ref, edge_ref, done_ref, acc_ref, q_buf, token_ref, x_ref, stage, h_buf, w_buf, z_buf, send_buf, edge_buf,
-                    x_sem, h_sem, w_sem, q_sem, send_sem, recv_sem, edge_send, edge_recv):
+                    x_sem, h_sem, first_sem, w_sem, q_sem, send_sem, recv_sem, edge_send, edge_recv):
     me = lax.axis_index("tp")
     vocab, depth = w_ref.shape
     groups, n_dev = recv_ref.shape[:2]
@@ -210,8 +210,13 @@
     def q_copy(g, j):
         return pltpu.make_async_copy(q_ref.at[j, pl.ds(pl.multiple_of(g * seqs, seqs), seqs)], q_buf.at[j], q_sem.at[j])
 
+    def first_w(c):
+        rows = pl.ds(pl.multiple_of(c * LANE, LANE), LANE)
+        return pltpu.make_async_copy(w_ref.at[rows], w_buf.at[0, rows], first_sem.at[c])
+
+    first_w(0).start()
     h_start(0)
-    w_copy(0, TILE).start()
+    first_w(1).start()
     w_copy(1, TILE).start()
 
     barrier = pltpu.get_barrier_semaphore()
@@ -220,18 +225,15 @@
 
     pltpu.make_async_copy(x_in, x_ref, x_sem.at[0]).start()
     acc_ref[...] = jnp.zeros_like(acc_ref)
-    relayout(0)
-    h_start(1)
-    pl.semaphore_wait(barrier, n_dev - 1)
-
-    def send(g, t, width):
+
+    def send(g, t, first, width):
         for c in range(width):
-            recv_ref[g, me, t * lt + c] = send_buf[t, c, pl.ds(pl.multiple_of(me * seg, seg), seg), :]
+            recv_ref[g, me, t * lt + first + c] = send_buf[t, first + c, pl.ds(pl.multiple_of(me * seg, seg), seg), :]
         for k in ORDER:
             d = peer_of(me, k)
             pltpu.make_async_remote_copy(
-                src_ref=send_buf.at[t, pl.ds(0, width), pl.ds(pl.multiple_of(d * seg, seg), seg)],
-                dst_ref=recv_ref.at[g, me, pl.ds(t * lt, width)],
+                src_ref=send_buf.at[t, pl.ds(first, width), pl.ds(pl.multiple_of(d * seg, seg), seg)],
+                dst_ref=recv_ref.at[g, me, pl.ds(t * lt + first, width)],
                 send_sem=send_sem.at[t],
                 recv_sem=recv_sem.at[g, k - 1],
                 device_id={"tp": d},
@@ -266,6 +268,32 @@
 
     rest = full - (n_tiles - 1) * lt
 
+    def product(h, w):
+        return lax.dot_general(h, w, (((1,), (1,)), ((), ())), preferred_element_type=jnp.float32) * INV_TEMP
+
+    def by_position(t, c):
+        for d in range(n_dev):
+            for j in range(pos):
+                send_buf[t, c, pl.ds(d * seg + j * seqs, seqs), :] = z_buf[c, pl.ds(d * seg + j, seqs, stride=pos), :]
+
+    relayout(0)
+
+    def first_tile(c, carry):
+        first_w(c).wait()
+        z_buf[c] = product(h_buf[...], w_buf[0, pl.ds(pl.multiple_of(c * LANE, LANE), LANE)])
+        by_position(0, c)
+
+        @pl.when(c == 0)
+        def _():
+            h_start(1)
+            w_copy(2, TILE).start()
+            pl.semaphore_wait(barrier, n_dev - 1)
+
+        send(0, 0, c, 1)
+        return carry
+
+    lax.fori_loop(0, lt, first_tile, 0)
+
     def step(u, carry):
         g = u // n_tiles
         t = lax.rem(u, n_tiles)
@@ -285,7 +313,7 @@
         def _():
             on_tile(u + 2, lambda c: c.start())
 
-        z = lax.dot_general(h_buf[...], w_buf[slot], (((1,), (1,)), ((), ())), preferred_element_type=jnp.float32) * INV_TEMP
+        z = product(h_buf[...], w_buf[slot])
         for c in range(lt):
             z_buf[c] = z[:, c * LANE:(c + 1) * LANE]
 
@@ -298,22 +326,20 @@
             wait_sent(t, rest)
 
         for c in range(lt):
-            for d in range(n_dev):
-                for j in range(pos):
-                    send_buf[t, c, pl.ds(d * seg + j * seqs, seqs), :] = z_buf[c, pl.ds(d * seg + j, seqs, stride=pos), :]
+            by_position(t, c)
 
         @pl.when(t < n_tiles - 1)
         def _():
-            send(g, t, lt)
+            send(g, t, 0, lt)
 
         @pl.when(t == n_tiles - 1)
         def _():
-            send(g, t, rest)
+            send(g, t, 0, rest)
             send_edge(g)
 
         return carry
 
-    lax.fori_loop(0, n_steps, step, 0)
+    lax.fori_loop(1, n_steps, step, 0)
 
     def wait_group(g):
         for k in ORDER:
@@ -488,6 +514,7 @@
                 pltpu.VMEM((groups, n, SEQS, LANE), jnp.float32),
                 dma((1,)),
                 dma((depth // LANE // H_PART,)),
+                dma((TILE // LANE,)),
                 dma((SLOTS,)),
                 dma((draft,)),
                 dma((n_tiles,)),

time: 193 us -> 193 us (level)
  no operation moved by 1% of the time
where the time goes in v7:
time: 193 us
  Pallas kernels  192 us (99%)
    pallas_call x1, Pallas kernels, local_step(): pl.pallas_call(exchange_kernel, out_shape=[pltpu.VMEM((groups, n, full, S...  186 us
    pallas_call x1, Pallas kernels, local_step(): pl.pallas_call(output_kernel, out_shape=[jax.ShapeDtypeStruct((draft, seq...  5.89 us

profile of v7, /device:TPU:0, one launch (start us, length us, event | category | flops | bytes accessed | tf_op | source)
XLA Modules:
  0.0 192.8 jit_solution(8813588139997108566)
XLA Ops:
  0.6 186.3 %logits_exchange.1 = (f32[4,8,31,32,128]{4,3,2,1,0:T(8,128)S(1)}, f32[4,8,8,128]{3,2,1,0:T(8,128)S(1)}, f32[3,4,8,32000]{3,2,1,0:T(8,128)S(1)}, f32[4,32]{1,0:T(...) custom-call(s32[3,256]{1,0:T(4,128)} %bitcast.11, bf16[8,32,4,8192]{3,2,1,0:T(4,128)(2,1)} %bitcast.8, ...), custom_call_target="tpu_custom_call" | custom-call | flops 67108864000 | bytes 65536000 | tf_op jit(solution)/shard_map/logits_exchange/pallas_call | solution.py:495
  186.9 5.9 %write_outputs.1 = (f32[3,32,32000]{2,1,0:T(8,128)}, f32[32,32000]{1,0:T(8,128)}, f32[3,32]{1,0:T(4,128)}, f32[1,32]{1,0:T(1,128)}) custom-call(f32[4,8,31,32,128]{4,3,2,1,0:T(8,128)S(1)} %get-tuple-element.14.recv_ref, f32[4,8,8,128]{3,2,1,0:T(8,128)S(1)} %get-tuple-element.15.edge_ref, f32[3,4,8,32000]{3,2,1,0:T(8,128)S(1)} %get-tuple-element.16.done_ref, ...), custom_call_target="tpu_custom_call" | custom-call | tf_op jit(solution)/shard_map/write_outputs/pallas_call | solution.py:530

commit v8 on v7

--- a/solution.py
+++ b/solution.py
@@ -128,12 +128,12 @@
     return jnp.minimum(1.0, jnp.sum(p_pick, axis=1, keepdims=True) / jnp.sum(q_pick, axis=1, keepdims=True))
 
 
-def residual_rows(get, put, q_tile, inv, scale, n_g):
+def residual_rows(get, put, q_tile, inv, scale, first, last):
     def body(i, carry):
         put(i, jnp.maximum(get(i) * inv - q_tile(i), 0.0) * scale)
         return carry
 
-    lax.fori_loop(0, n_g // WIDE, body, 0)
+    lax.fori_loop(first, last, body, 0)
 
 
 def to_lanes(col, first, n_out):
@@ -386,7 +386,7 @@
             x = token_tile(lambda b: x_ref[j, me * per_dev + g * seqs + b], seqs)
             scale, accept = excess_rows_with_picks(get, q_tile, x, inv, n_g)
             accepts.append(accept)
-            residual_rows(get, put_wide, q_tile, inv, scale, n_g)
+            residual_rows(get, put_wide, q_tile, inv, scale, 0, n_g // WIDE)
 
             q_copy(g + 1, j).start()
 
@@ -453,14 +453,19 @@
         inv = softmax_rows(tile, edge, put, n_dev, full, tail, seqs)
         if j == draft:
             finish_bonus(get, put_wide, inv, n_g)
+            out(g_last, j, row_buf.at[j]).start()
         else:
             def q_tile(i):
                 return q_buf[j, :, chunk(i)]
 
             scale, accept = excess_rows_with_picks(get, q_tile, token_ref[j], inv, n_g)
             accepts.append(accept)
-            residual_rows(get, put_wide, q_tile, inv, scale, n_g)
-        out(g_last, j, row_buf.at[j]).start()
+            half = n_g // WIDE // 2
+            for first, last in ((0, half), (half, n_g // WIDE)):
+                residual_rows(get, put_wide, q_tile, inv, scale, first, last)
+                cols = pl.ds(first * WIDE * LANE, (last - first) * WIDE * LANE)
+                dst = res_ref.at[j, pl.ds(g_last * seqs, seqs), cols]
+                pltpu.make_async_copy(row_buf.at[j, :, cols], dst, out_sem.at[g_last, j]).start()
 
     for j in range(draft):
         acc_buf[j:j + 1, :] = part_ref[j:j + 1, :] + to_lanes(accepts[j], g_last * seqs, per_dev)

time: 193 us -> 193 us (level)
  no operation moved by 1% of the time
where the time goes in v8:
time: 193 us
  Pallas kernels  192 us (99%)
    pallas_call x1, Pallas kernels, local_step(): pl.pallas_call(exchange_kernel, out_shape=[pltpu.VMEM((groups, n, full, S...  186 us
    pallas_call x1, Pallas kernels, local_step(): pl.pallas_call(output_kernel, out_shape=[jax.ShapeDtypeStruct((draft, seq...  5.87 us

profile of v8, /device:TPU:0, one launch (start us, length us, event | category | flops | bytes accessed | tf_op | source)
XLA Modules:
  0.0 192.8 jit_solution(14127795008542744971)
XLA Ops:
  0.6 186.3 %logits_exchange.1 = (f32[4,8,31,32,128]{4,3,2,1,0:T(8,128)S(1)}, f32[4,8,8,128]{3,2,1,0:T(8,128)S(1)}, f32[3,4,8,32000]{3,2,1,0:T(8,128)S(1)}, f32[4,32]{1,0:T(...) custom-call(s32[3,256]{1,0:T(4,128)} %bitcast.11, bf16[8,32,4,8192]{3,2,1,0:T(4,128)(2,1)} %bitcast.8, ...), custom_call_target="tpu_custom_call" | custom-call | flops 67108864000 | bytes 65536000 | tf_op jit(solution)/shard_map/logits_exchange/pallas_call | solution.py:500
  186.9 5.9 %write_outputs.1 = (f32[3,32,32000]{2,1,0:T(8,128)}, f32[32,32000]{1,0:T(8,128)}, f32[3,32]{1,0:T(4,128)}, f32[1,32]{1,0:T(1,128)}) custom-call(f32[4,8,31,32,128]{4,3,2,1,0:T(8,128)S(1)} %get-tuple-element.14.recv_ref, f32[4,8,8,128]{3,2,1,0:T(8,128)S(1)} %get-tuple-element.15.edge_ref, f32[3,4,8,32000]{3,2,1,0:T(8,128)S(1)} %get-tuple-element.16.done_ref, ...), custom_call_target="tpu_custom_call" | custom-call | tf_op jit(solution)/shard_map/write_outputs/pallas_call | solution.py:535
